TPU v7x, 128 devices: a whole 4x4x4 slice. The times are simulated.
128 devices in a mesh: rep: 8 (over y_lo, z), inst: 16 (over y_hi, x, core).
Axes of the slice: x: 4, y: 4 (y_hi: 2, y_lo: 2; y = y_hi * 2 + y_lo), z: 4, core: 2. Of those that a mesh axis runs over, the one named last changes fastest.
Arguments:
- acts: bfloat16 [131072, 4096], P(('rep', 'inst')), may hold values from -6 to 6
- grad_keys: bfloat16 [131072, 1024], P(('rep', 'inst')), may hold values from -0.03125 to 0.03125
- grad_values: bfloat16 [131072, 1024], P(('rep', 'inst')), may hold values from -0.03125 to 0.03125
- grad_logits: bfloat16 [8, 131072], P(None, ('rep', 'inst')), may hold values from -0.03125 to 0.03125
- order: int32 [32], replicated, may hold values from 0 to 31, each once
- bucket_param: float32 [4, 2048, 1024], P(None, 'inst'), may hold values from -6 to 6
- bucket_m: float32 [4, 2048, 1024], P(None, 'inst'), may hold values from -6 to 6
- bucket_v: float32 [4, 2048, 1024], P(None, 'inst'), may hold values from 0.25 to 4
- router_param: float32 [32, 1024], P('inst'), may hold values from -6 to 6
- router_m: float32 [32, 1024], P('inst'), may hold values from -6 to 6
- router_v: float32 [32, 1024], P('inst'), may hold values from 0.25 to 4
Outputs:
- new_param: float32 [4, 2048, 1024], P(None, 'inst')
- new_moment: float32 [4, 2048, 1024], P(None, 'inst')
- new_second: float32 [4, 2048, 1024], P(None, 'inst')
- router_new_param: float32 [32, 1024], P('inst')
- router_new_moment: float32 [32, 1024], P('inst')
- router_new_second: float32 [32, 1024], P('inst')
Inputs may be any that keep to these rules, and one draw needn't show every extreme that they name: order is a permutation of the 32 row blocks; entries with k * 8 <= s < (k + 1) * 8 fill bucket k.
All inputs are finite; a program needn't handle non-finite values.
Results may differ from a plain program's by a relative error of at most 0.0003.
Values sent between devices are 32-bit elements; how exact they have to be, the bound alone decides.
A program may use at most 256 MiB of HBM per device.

v0:
```python
import jax
import jax.numpy as jnp
from jax import lax
from jax.sharding import PartitionSpec as P

BUCKETS = 4
BLOCK_ROWS = 256


beta_first = 0.9
beta_second = 0.95
step_rate = 0.05
decay_rate = 0.1
epsilon = 1e-08
correct_first = 1.0 - 0.9**10
correct_second = 1.0 - 0.95**10


def copy_for_each(shard, axis):
    copies = jnp.broadcast_to(shard, (lax.axis_size(axis), *shard.shape))
    return lax.all_to_all(copies, axis, split_axis=0, concat_axis=0, tiled=True)


def over_copies(shard, axis):
    everything = copy_for_each(shard, axis)
    return jnp.sum(everything, axis=0)


def split_up(shard, dim, devices):
    shape = shard.shape
    blocks = shard.reshape(*shape[:dim], devices, shape[dim] // devices, *shape[dim + 1 :])
    return jnp.moveaxis(blocks, dim, 0)


def sent_and_summed(shard, axis, dim):
    devices = lax.axis_size(axis)
    blocks = lax.all_to_all(split_up(shard, dim, devices), axis, 0, 0, tiled=True)
    return jnp.sum(blocks, axis=0)


def contract(left, right):
    return lax.dot_general(
        left, right, (((0,), (0,)), ((), ())), preferred_element_type=jnp.float32
    )


def adamw(grad, param, moment, second):
    moment_new = beta_first * moment + (1.0 - beta_first) * grad
    second_new = beta_second * second + (1.0 - beta_second) * grad * grad
    ratio = moment_new / correct_first / (jnp.sqrt(second_new / correct_second) + epsilon)
    param_new = param - step_rate * (ratio + decay_rate * param)
    return (param_new, moment_new, second_new)


def owner_step(term, param, moment, second):
    share = lax.psum_scatter(term, "inst", scatter_dimension=0, tiled=True)
    total = over_copies(share, "rep")
    return adamw(total, param, moment, second)


def on_device(
    acts,
    grad_keys,
    grad_values,
    grad_logits,
    order,
    bucket_param,
    bucket_m,
    bucket_v,
    router_param,
    router_m,
    router_v,
):
    width = acts.shape[1]
    per_matrix = width // BLOCK_ROWS
    per_bucket = order.shape[0] // BUCKETS
    upstream = jnp.stack([grad_keys, grad_values])
    params_out = []
    moments_out = []
    seconds_out = []
    for bucket in range(BUCKETS):
        pieces = []
        for slot in range(per_bucket):
            block = order[bucket * per_bucket + slot]
            which = block // per_matrix
            start = block % per_matrix * BLOCK_ROWS
            columns = lax.dynamic_slice_in_dim(acts, start, BLOCK_ROWS, 1)
            upstream_piece = lax.dynamic_index_in_dim(upstream, which, 0, keepdims=False)
            pieces.append(contract(columns, upstream_piece))
        term = jnp.concatenate(pieces, axis=0)
        fresh = owner_step(term, bucket_param[bucket], bucket_m[bucket], bucket_v[bucket])
        params_out.append(fresh[0])
        moments_out.append(fresh[1])
        seconds_out.append(fresh[2])
    router_term = jnp.dot(grad_logits, acts, preferred_element_type=jnp.float32)
    router_term = router_term.reshape(-1, router_param.shape[1])
    router_share = sent_and_summed(router_term, "inst", 0)
    router_total = over_copies(router_share, "rep")
    router_fresh = adamw(router_total, router_param, router_m, router_v)
    return (
        jnp.stack(params_out),
        jnp.stack(moments_out),
        jnp.stack(seconds_out),
        router_fresh[0],
        router_fresh[1],
        router_fresh[2],
    )


def solution(mesh):
    return jax.shard_map(
        on_device,
        mesh=mesh,
        in_specs=(
            P(("rep", "inst"), None),
            P(("rep", "inst"), None),
            P(("rep", "inst"), None),
            P(None, ("rep", "inst")),
            P(),
            P(None, "inst", None),
            P(None, "inst", None),
            P(None, "inst", None),
            P("inst", None),
            P("inst", None),
            P("inst", None),
        ),
        out_specs=(
            P(None, "inst", None),
            P(None, "inst", None),
            P(None, "inst", None),
            P("inst", None),
            P("inst", None),
            P("inst", None),
        ),
        check_vma=False,
    )
```

profile of v0, /device:TPU:0, one launch (start us, length us, event | category | flops | bytes accessed | tf_op | source)
XLA Modules:
  0.0 593.3 jit_solution(14816835825647760448)
XLA Ops:
  31.7 4.1 fusion.218
  35.8 3.3 fusion.215
  55.3 3.3 fusion.197
  79.2 4.4 fusion.194
  93.4 3.3 fusion.182
  96.7 3.3 fusion.179
  126.4 4.1 fusion.146
  130.6 3.3 fusion.143
  174.4 4.2 fusion.170
  181.9 3.3 fusion.164
  185.2 3.3 fusion.161
  188.5 3.4 fusion.158
  191.9 3.3 fusion.155
  201.7 5.3 fusion.340
  207.2 15.2 %all_to_all.30 = f32[16,2,1024]{2,1,0:T(2,128)S(1)} all-to-all(f32[16,2,1024]{2,1,0:T(2,128)S(1)} %reshape_reshape.3), channel_id=1, replica_groups=mesh['rep'=8,'inst'=16] {'inst'}, dimensions={0} | all-to-all | bytes 262144 | tf_op jit(solution)/shard_map/all_to_all | solution.py:37
  222.4 11.8 %all_to_all.31 = f32[8,2,1024]{2,1,0:T(2,128)S(1)} all-to-all(f32[8,2,1024]{2,1,0:T(2,128)S(1)} %broadcast_in_dim.19), channel_id=1, replica_groups=mesh['rep'=8,'inst'=16] {'rep'}, dimensions={0} | all-to-all | bytes 131072 | tf_op jit(solution)/shard_map/all_to_all | solution.py:21
  234.3 3.5 broadcast_in_dim.15
  237.8 4.5 all-to-all-start
  242.4 33.2 %reduce-scatter.7.cloned.1.call-done = f32[128,1024]{1,0:T(8,128)} async-done(((f32[2048,1024]{1,0:T(8,128)}), f32[128,1024]{1,0:T(8,128)}) %reduce-scatter.7.cloned.1.call-update) | async-done | bytes 524304 | tf_op jit(solution)/shard_map/reduce_scatter | solution.py:56
  275.6 19.4 %all-to-all-done = f32[8,128,1024]{2,1,0:T(8,128)} async-done(((f32[8,128,1024]{2,1,0:T(8,128)}), f32[8,128,1024]{2,1,0:T(8,128)}, u32[]{:S(2)}, u32[]{:S(2)}) %all-to-all-start) | async-done | bytes 4194336 | tf_op jit(solution)/shard_map/all_to_all | solution.py:21
  295.0 3.6 broadcast_in_dim.16
  298.6 4.6 all-to-all-start.1
  303.2 100.3 %reduce-scatter.11.cloned.1.call-done = f32[128,1024]{1,0:T(8,128)} async-done(((f32[2048,1024]{1,0:T(8,128)}), f32[128,1024]{1,0:T(8,128)}) %reduce-scatter.11.cloned.1.call-update) | async-done | bytes 524304 | tf_op jit(solution)/shard_map/reduce_scatter | solution.py:56
  403.5 3.5 broadcast_in_dim.18
  407.0 4.9 all-to-all-start.3
  411.9 107.2 %reduce-scatter.9.cloned.1.call-done = f32[128,1024]{1,0:T(8,128)} async-done(((f32[2048,1024]{1,0:T(8,128)}), f32[128,1024]{1,0:T(8,128)}) %reduce-scatter.9.cloned.1.call-update) | async-done | bytes 524304 | tf_op jit(solution)/shard_map/reduce_scatter | solution.py:56
  519.2 3.5 broadcast_in_dim.17
  522.7 4.7 all-to-all-start.2
  533.3 3.4 reduce_sum.68
  536.7 37.9 %all-to-all-done.2 = f32[8,128,1024]{2,1,0:T(8,128)} async-done(((f32[8,128,1024]{2,1,0:T(8,128)}), f32[8,128,1024]{2,1,0:T(8,128)}, u32[]{:S(2)}, u32[]{:S(2)}) %all-to-all-start.2) | async-done | bytes 4194336 | tf_op jit(solution)/shard_map/all_to_all | solution.py:21
  574.6 3.4 reduce_sum.66
  578.0 4.1 multiply_subtract_fusion.3
  (61 shorter events, 76.9 us)
Async XLA Ops:
  7.2 194.5 %copy-start = (bf16[8,1024]{1,0:T(8,128)(2,1)S(1)}, bf16[8,1024]{1,0:T(8,128)(2,1)}, u32[]{:S(2)}) copy-start(bf16[8,1024]{1,0:T(8,128)(2,1)} %param.14) | copy-start | bytes 49156
  7.2 227.1 %reduce-scatter.5.cloned.1.call-start = ((), (), s32[]{:S(2)}) async-start(), calls=%async_computation.10 | async-start | bytes 8912896 | tf_op jit(solution)/shard_map/reduce_scatter | solution.py:56
  31.6 4.1 copy-start.5
  31.7 4.1 copy-start.6
  58.6 217.0 %reduce-scatter.7.cloned.1.call-start = ((), (), s32[]{:S(2)}) async-start(), calls=%async_computation.11 | async-start | bytes 8912896 | tf_op jit(solution)/shard_map/reduce_scatter | solution.py:56
  79.2 4.4 copy-start.7
  106.5 297.0 %reduce-scatter.11.cloned.1.call-start = ((), (), s32[]{:S(2)}) async-start(), calls=%async_computation.13 | async-start | bytes 8912896 | tf_op jit(solution)/shard_map/reduce_scatter | solution.py:56
  126.4 4.1 copy-start.8
  153.4 365.8 %reduce-scatter.9.cloned.1.call-start = ((), (), s32[]{:S(2)}) async-start(), calls=%async_computation.12 | async-start | bytes 8912896 | tf_op jit(solution)/shard_map/reduce_scatter | solution.py:56
  174.4 4.2 copy-start.9
  237.8 57.1 %all-to-all-start = ((f32[8,128,1024]{2,1,0:T(8,128)}), f32[8,128,1024]{2,1,0:T(8,128)}, u32[]{:S(2)}, u32[]{:S(2)}) async-start(f32[8,128,1024]{2,1,0:T(8,128)} %broadcast_in_dim.15), calls=%async_computation.1 | async-start | bytes 8388608 | tf_op jit(solution)/shard_map/all_to_all | solution.py:21
  298.6 105.0 %all-to-all-start.1 = ((f32[8,128,1024]{2,1,0:T(8,128)}), f32[8,128,1024]{2,1,0:T(8,128)}, u32[]{:S(2)}, u32[]{:S(2)}) async-start(f32[8,128,1024]{2,1,0:T(8,128)} %broadcast_in_dim.16), calls=%async_computation.3 | async-start | bytes 8388608 | tf_op jit(solution)/shard_map/all_to_all | solution.py:21
  407.0 112.1 %all-to-all-start.3 = ((f32[8,128,1024]{2,1,0:T(8,128)}), f32[8,128,1024]{2,1,0:T(8,128)}, u32[]{:S(2)}, u32[]{:S(2)}) async-start(f32[8,128,1024]{2,1,0:T(8,128)} %broadcast_in_dim.18), calls=%async_computation.7 | async-start | bytes 8388608 | tf_op jit(solution)/shard_map/all_to_all | solution.py:21
  522.7 4.7 copy-start.2
  522.7 4.7 copy-start.3
  522.7 4.8 copy-start.4
  522.7 51.9 %all-to-all-start.2 = ((f32[8,128,1024]{2,1,0:T(8,128)}), f32[8,128,1024]{2,1,0:T(8,128)}, u32[]{:S(2)}, u32[]{:S(2)}) async-start(f32[8,128,1024]{2,1,0:T(8,128)} %broadcast_in_dim.17), calls=%async_computation.5 | async-start | bytes 8388608 | tf_op jit(solution)/shard_map/all_to_all | solution.py:21
  536.7 41.3 %copy-start.1 = (f32[4,128,1024]{2,1,0:T(8,128)S(1)}, f32[4,128,1024]{2,1,0:T(8,128)}, u32[]{:S(2)}) copy-start(f32[4,128,1024]{2,1,0:T(8,128)} %param.16) | copy-start | bytes 6291460
Sparse Core Ops, SparseCore 0:
  58.7 104.8 reduce-scatter.4
  167.9 107.5 reduce-scatter.6
  279.9 123.5 reduce-scatter.10
  407.7 111.4 reduce-scatter.8
where the time goes:
time: 603 us; the launch traced here: 593 us
  waiting for transfers between devices  298 us (49%)
  matrix products  114 us (19%)
  between operations  95.7 us (16%)
  blocking collectives  27 us (4%)
  other arithmetic  21 us (3%)
  starting transfers between devices  19.5 us (3%)
  local copies, waits for them, and re-layouts  18.3 us (3%)
    reduce_scatter x4, waiting for transfers between devices, owner_step(): share = lax.psum_scatter(term, 'inst', scatter_dimension=0, tiled=True)  241 us
    dot_general x32, matrix products, contract(): lax.dot_general(left, right, (((0,), (0,)), ((), ())), preferred_element_...  108 us
    all_to_all x4, waiting for transfers between devices, copy_for_each(): return lax.all_to_all(copies, axis, split_axis=0, concat_axis=0, tiled=True)  57.3 us
    all_to_all x4, starting transfers between devices, copy_for_each(): return lax.all_to_all(copies, axis, split_axis=0, concat_axis=0, tiled=True)  18.7 us
    all_to_all x1, blocking collectives, sent_and_summed(): lax.all_to_all(split_up(shard, dim, devices), axis, 0, 0, tiled=True)  15.2 us
    broadcast_in_dim x5, local copies, waits for them, and re-layouts, copy_for_each(): copies = jnp.broadcast_to(shard, (lax.axis_size(axis), *shard.shape))  14.2 us
  transfers between devices with their start and end apart: 8, of which 5 were waited for; matrix products, arithmetic and copies ran while one was open for 18% of the time, Pallas kernels for 0%

commit v1 on v0

v1 whole, which is shorter than its diff:
```python
import jax
import jax.numpy as jnp
from jax import lax
from jax.experimental import pallas as pl
from jax.experimental.pallas import tpu as pltpu
from jax.sharding import PartitionSpec as P

BUCKETS = 4
BLOCK_ROWS = 256
STEPS = 8
HALF = 512

beta_first = 0.9
beta_second = 0.95
step_rate = 0.05
decay_rate = 0.1
epsilon = 1e-08
correct_first = 1.0 - 0.9**10
correct_second = 1.0 - 0.95**10

MESH = pl.DeviceIdType.MESH
F32 = jnp.float32

DIMS = (("x", "y", "z"), ("y", "z", "x"), ("z", "x", "y"))
WIDTH = ((256, 128, 128), (128, 256, 128))
OFFSET = ((0, 256, 384), (256, 0, 384))


def adamw(grad, param, moment, second):
    moment_new = beta_first * moment + (1.0 - beta_first) * grad
    second_new = beta_second * second + (1.0 - beta_second) * grad * grad
    ratio = moment_new / correct_first / (jnp.sqrt(second_new / correct_second) + epsilon)
    param_new = param - step_rate * (ratio + decay_rate * param)
    return (param_new, moment_new, second_new)


def scratch():
    tree = {
        "acts": pltpu.VMEM((16, 1024, BLOCK_ROWS), jnp.bfloat16),
        "grads": pltpu.VMEM((2, 1024, 1024), jnp.bfloat16),
        "turned": pltpu.VMEM((BLOCK_ROWS, 1024), jnp.bfloat16),
        "out": pltpu.VMEM((BUCKETS, 2, 2, 4, 16, HALF), F32),
        "rt": pltpu.VMEM((2, 4, 2, 1, 2048), F32),
        "rx": pltpu.VMEM((4, 2, 1, 2048), F32),
        "rxx": pltpu.VMEM((3, 2, 1, 2048), F32),
        "rxy": pltpu.VMEM((4, 1, 2048), F32),
        "rxz": pltpu.VMEM((4, 1, 2048), F32),
        "ry": pltpu.VMEM((2, 1, 2048), F32),
        "load_sem": pltpu.SemaphoreType.DMA((18,)),
        "x_send": pltpu.SemaphoreType.DMA((STEPS, 3)),
        "x_recv": pltpu.SemaphoreType.DMA((STEPS, 3)),
        "p1_send": pltpu.SemaphoreType.DMA((STEPS, 3, 6)),
        "p1_recv": pltpu.SemaphoreType.DMA((STEPS, 3, 6)),
        "p2_send": pltpu.SemaphoreType.DMA((STEPS, 3, 6)),
        "p2_recv": pltpu.SemaphoreType.DMA((STEPS, 3, 6)),
        "p3_send": pltpu.SemaphoreType.DMA((STEPS, 3, 3)),
        "p3_recv": pltpu.SemaphoreType.DMA((STEPS, 3, 3)),
        "ag_send": pltpu.SemaphoreType.DMA((STEPS, 5)),
        "ag_recv": pltpu.SemaphoreType.DMA((STEPS, 5)),
        "r_send": pltpu.SemaphoreType.DMA((10,)),
        "r_recv": pltpu.SemaphoreType.DMA((10,)),
        "out_sem": pltpu.SemaphoreType.DMA((STEPS,)),
    }
    for parity in range(2):
        for colour in range(3):
            w = WIDTH[parity][colour]
            tail = f"{parity}{colour}"
            tree["px" + tail] = pltpu.VMEM((2, 4, 4, 4, 16, w), F32)
            tree["xr" + tail] = pltpu.VMEM((2, 4, 4, 4, 16, w), F32)
            tree["ra" + tail] = pltpu.VMEM((BUCKETS, 6, 2, 4, 16, w), F32)
            tree["q" + tail] = pltpu.VMEM((BUCKETS, 4, 4, 16, w), F32)
            tree["rb" + tail] = pltpu.VMEM((BUCKETS, 6, 2, 16, w), F32)
            tree["rc" + tail] = pltpu.VMEM((BUCKETS, 3, 16, w), F32)
    return tree


def kernel(names, order, logits, acts_hbm, keys_hbm, values_hbm, out_hbm, router_out, *refs):
    ref = dict(zip(names, refs))
    rep = lax.axis_index("rep")
    inst = lax.axis_index("inst")
    yl, z = rep // 4, rep % 4
    yh, x, core = inst // 8, (inst // 2) % 4, inst % 2
    place = {"x": x, "y": yh * 2 + yl, "z": z, "c": core}

    def device(**change):
        at = {**place, **change}
        y = at["y"]
        return {"rep": (y % 2) * 4 + at["z"], "inst": ((y // 2) * 4 + at["x"]) * 2 + at["c"]}

    def along(dim, delta):
        return device(**{dim: (place[dim] + delta) % 4})

    sibling = device(c=1 - core)
    partner = device(y=yh * 2 + (1 - yl))

    def send(src, dst, send_sem, recv_sem, to):
        copy = pltpu.make_async_remote_copy(
            src_ref=src, dst_ref=dst, send_sem=send_sem, recv_sem=recv_sem, device_id=to, device_id_type=MESH
        )
        copy.start()

    def wait_recv(dst, sem):
        pltpu.make_async_copy(dst, dst, sem).wait()

    wait_send = wait_recv

    loads = []
    for i in range(16):
        loads.append(
            pltpu.make_async_copy(
                acts_hbm.at[:, i * BLOCK_ROWS : (i + 1) * BLOCK_ROWS], ref["acts"].at[i], ref["load_sem"].at[i]
            )
        )
    loads.append(pltpu.make_async_copy(keys_hbm, ref["grads"].at[0], ref["load_sem"].at[16]))
    loads.append(pltpu.make_async_copy(values_hbm, ref["grads"].at[1], ref["load_sem"].at[17]))
    for load in loads:
        load.start()

    barrier = pltpu.get_barrier_semaphore()
    peers = [sibling] + [along(d, delta) for d in "xyz" for delta in (1, 2, 3)]
    for peer in peers:
        pl.semaphore_signal(barrier, inc=1, device_id=peer, device_id_type=MESH)

    for i in range(16):
        loads[i].wait()
        term = jnp.dot(logits[...], ref["acts"][i], preferred_element_type=F32)
        for e in range(8):
            ref["rt"][i // 8, e % 4, e // 4, :, pl.ds((i % 8) * 256, 256)] = term[e : e + 1, :]
    loads[16].wait()
    loads[17].wait()

    def matmul(step, first, last):
        bucket, parity = step // 2, step % 2

        def body(j, carry):
            slot_y, slot_x = j // 4, j % 4
            block = order[bucket * 8 + j]
            ref["turned"][...] = ref["acts"][block % 16].T
            for n in range(2):
                lo = n * 256
                piece = jnp.dot(
                    ref["turned"][...],
                    ref["grads"][block // 16, :, parity * HALF + lo : parity * HALF + lo + 256],
                    preferred_element_type=F32,
                )
                for colour in range(3):
                    w, off = WIDTH[parity][colour], OFFSET[parity][colour]
                    if not lo <= off < lo + 256:
                        continue
                    px = ref[f"px{parity}{colour}"]
                    part = piece[:, off - lo : off - lo + w]
                    for h in range(2):
                        for l in range(2):
                            rows = part[h * 128 + l * 64 : h * 128 + l * 64 + 64].reshape(4, 16, w)
                            y = slot_y * 2 + l
                            if colour == 0:
                                px[h, slot_x, y] = rows
                            elif colour == 1:
                                for k in range(4):
                                    px[h, y, k, slot_x] = rows[k]
                            else:
                                for k in range(4):
                                    px[h, k, slot_x, y] = rows[k]
            return carry

        lax.fori_loop(first, last, body, 0)

    def exchange(step):
        b, par = step // 2, step % 2
        for q in range(3):
            send(
                ref[f"px{par}{q}"].at[1 - core],
                ref[f"xr{par}{q}"].at[b % 2],
                ref["x_send"].at[step, q],
                ref["x_recv"].at[step, q],
                sibling,
            )

    def add_sibling(step):
        b, par = step // 2, step % 2
        for q in range(3):
            px, xr = ref[f"px{par}{q}"], ref[f"xr{par}{q}"]
            wait_recv(xr.at[b % 2], ref["x_recv"].at[step, q])

            def body(d, carry):
                px[core, d] = px[core, d] + xr[b % 2, d]
                return carry

            lax.fori_loop(0, 4, body, 0)

    def views(step, q, phase):
        b, par = step // 2, step % 2
        if phase == 1:
            px, recv = ref[f"px{par}{q}"], ref[f"ra{par}{q}"]
            return px, (lambda d, h: (core, d, pl.ds(2 * h, 2))), recv, b
        src, recv = ref[f"q{par}{q}"], ref[f"rb{par}{q}"]
        return src, (lambda d, h: (b, d, pl.ds(2 * h, 2))), recv, b

    def ring_send(step, q, phase, m, where, delta):
        src, at, recv, b = views(step, q, phase)
        dim = DIMS[q][phase - 1]
        d, h = where
        send(
            src.at[at((place[dim] + d) % 4, h)],
            recv.at[b, m],
            ref[f"p{phase}_send"].at[step, q, m],
            ref[f"p{phase}_recv"].at[step, q, m],
            along(dim, delta),
        )

    def ring_start(step, phase):
        for q in range(3):
            ring_send(step, q, phase, 0, (2, 0), 1)
            ring_send(step, q, phase, 1, (2, 1), 3)
            ring_send(step, q, phase, 2, (1, 1), 1)
            ring_send(step, q, phase, 3, (3, 0), 3)

    def ring_relay(step, phase):
        for q in range(3):
            src, at, recv, b = views(step, q, phase)
            here = place[DIMS[q][phase - 1]]
            for m, d, h in ((0, 1, 0), (1, 3, 1)):
                wait_recv(recv.at[b, m], ref[f"p{phase}_recv"].at[step, q, m])
                spot = at((here + d) % 4, h)
                src[spot] = src[spot] + recv[b, m]
                ring_send(step, q, phase, 4 + m, (d, h), d)

    def ring_end(step, phase):
        b, par = step // 2, step % 2
        for q in range(3):
            src, at, recv, _ = views(step, q, phase)
            here = place[DIMS[q][phase - 1]]
            for h, arrived in ((0, (3, 4)), (1, (2, 5))):
                for m in arrived:
                    wait_recv(recv.at[b, m], ref[f"p{phase}_recv"].at[step, q, m])
                spot = at(here, h)
                total = src[spot] + recv[b, arrived[0]] + recv[b, arrived[1]]
                if phase == 1:
                    ref[f"q{par}{q}"][b, pl.ds(2 * h, 2)] = total
                else:
                    src[spot] = total

    def ring_sent(step, phase):
        for q in range(3):
            recv = views(step, q, phase)[2]
            for m in range(6):
                wait_send(recv.at[step // 2, m], ref[f"p{phase}_send"].at[step, q, m])

    def exchange_sent(step):
        for q in range(3):
            wait_send(ref[f"xr{step % 2}{q}"].at[step // 2 % 2], ref["x_send"].at[step, q])

    def last_start(step):
        b, par = step // 2, step % 2
        for q in range(3):
            second, third = DIMS[q][1:]
            for m in range(3):
                delta = (1, 3, 2)[m]
                send(
                    ref[f"q{par}{q}"].at[b, place[second], (place[third] + delta) % 4],
                    ref[f"rc{par}{q}"].at[b, m],
                    ref["p3_send"].at[step, q, m],
                    ref["p3_recv"].at[step, q, m],
                    along(third, delta),
                )

    def last_end(step):
        b, par = step // 2, step % 2
        for q in range(3):
            second, third = DIMS[q][1:]
            rc = ref[f"rc{par}{q}"]
            for m in range(3):
                wait_recv(rc.at[b, m], ref["p3_recv"].at[step, q, m])
            total = ref[f"q{par}{q}"][b, place[second], place[third]] + rc[b, 0] + rc[b, 1] + rc[b, 2]
            ref["out"][b, par, yl, z, :, pl.ds(OFFSET[par][q], WIDTH[par][q])] = total

    def last_sent(step):
        for q in range(3):
            for m in range(3):
                wait_send(ref[f"rc{step % 2}{q}"].at[step // 2, m], ref["p3_send"].at[step, q, m])

    def gather_send(step, n, spot, to):
        out = ref["out"].at[(step // 2, step % 2) + spot]
        send(out, out, ref["ag_send"].at[step, n], ref["ag_recv"].at[step, n], to)

    def gather_wait(step, n, spot, which="ag_recv"):
        wait_recv(ref["out"].at[(step // 2, step % 2) + spot], ref[which].at[step, n])

    both = pl.ds(0, 2)

    def gather_partner(step):
        gather_send(step, 0, (yl, z), partner)

    def gather_start(step):
        gather_wait(step, 0, (1 - yl, z))
        gather_send(step, 1, (both, z), along("z", 1))
        gather_send(step, 2, (both, z), along("z", 3))

    def gather_relay(step):
        gather_wait(step, 1, (both, (z + 3) % 4))
        gather_send(step, 3, (0, (z + 3) % 4), along("z", 1))
        gather_wait(step, 2, (both, (z + 1) % 4))
        gather_send(step, 4, (1, (z + 1) % 4), along("z", 3))

    def gather_end(step):
        gather_wait(step, 3, (0, (z + 2) % 4))
        gather_wait(step, 4, (1, (z + 2) % 4))
        b, par = step // 2, step % 2
        pltpu.make_async_copy(
            ref["out"].at[b, par], out_hbm.at[b, :, :, :, pl.ds(par * HALF, HALF)], ref["out_sem"].at[step]
        ).start()

    def gather_sent(step):
        for n, spot in enumerate(((yl, z), (both, z), (both, z), (0, z), (1, z))):
            gather_wait(step, n, spot, "ag_send")
        b, par = step // 2, step % 2
        pltpu.make_async_copy(
            ref["out"].at[b, par], out_hbm.at[b, :, :, :, pl.ds(par * HALF, HALF)], ref["out_sem"].at[step]
        ).wait()

    def router_send(n, src, dst, to):
        send(src, dst, ref["r_send"].at[n], ref["r_recv"].at[n], to)

    def router_wait(n, dst):
        wait_recv(dst, ref["r_recv"].at[n])

    def router_0():
        router_send(0, ref["rt"].at[1 - core], ref["rx"], sibling)

    def router_1():
        router_wait(0, ref["rx"])
        ref["rt"][core] = ref["rt"][core] + ref["rx"][...]
        for m, delta in enumerate((1, 2, 3)):
            router_send(1 + m, ref["rt"].at[core, (x + delta) % 4], ref["rxx"].at[m], along("x", delta))

    def router_2():
        for m in range(3):
            router_wait(1 + m, ref["rxx"].at[m])
        ref["ry"][...] = ref["rt"][core, x] + ref["rxx"][0] + ref["rxx"][1] + ref["rxx"][2]
        here = place["y"]
        ref["rxy"][here] = ref["ry"][yh]
        for m, delta in enumerate((1, 2, 3)):
            to = (here + delta) % 4
            router_send(4 + m, ref["ry"].at[to // 2], ref["rxy"].at[here], along("y", delta))

    def router_3():
        here = place["y"]
        for m, delta in enumerate((1, 2, 3)):
            router_wait(4 + m, ref["rxy"].at[(here - delta) % 4])
        total = ref["rxy"][0] + ref["rxy"][1] + ref["rxy"][2] + ref["rxy"][3]
        ref["rxz"][z] = total
        for m, delta in enumerate((1, 2, 3)):
            router_send(7 + m, ref["rxz"].at[z], ref["rxz"].at[z], along("z", delta))

    def router_4():
        for m, delta in enumerate((1, 2, 3)):
            router_wait(7 + m, ref["rxz"].at[(z - delta) % 4])
        router_out[...] = ref["rxz"][0] + ref["rxz"][1] + ref["rxz"][2] + ref["rxz"][3]

    def router_sent():
        wait_send(ref["rx"], ref["r_send"].at[0])
        for m in range(3):
            wait_send(ref["rxx"].at[m], ref["r_send"].at[1 + m])
            wait_send(ref["rxy"].at[m], ref["r_send"].at[4 + m])
            wait_send(ref["rxz"].at[m], ref["r_send"].at[7 + m])

    router_stages = {0: router_0, 1: router_1, 2: router_2, 3: router_3, 4: router_4}

    matmul(0, 0, 8)
    pl.semaphore_wait(barrier, len(peers))
    exchange(0)
    for i in range(STEPS + 4):
        def live(step):
            return 0 <= step < STEPS

        if live(i):
            add_sibling(i)
            ring_start(i, 1)
        if live(i - 1):
            ring_end(i - 1, 1)
            ring_start(i - 1, 2)
        if live(i - 2):
            ring_end(i - 2, 2)
            last_start(i - 2)
        if live(i - 3):
            gather_start(i - 3)
        if live(i - 4):
            gather_end(i - 4)
        if i in router_stages:
            router_stages[i]()
        if live(i + 1):
            if live(i - 1):
                exchange_sent(i - 1)
                ring_sent(i - 1, 1)
            matmul(i + 1, 0, 8)
            exchange(i + 1)
        if live(i):
            ring_relay(i, 1)
        if live(i - 1):
            ring_relay(i - 1, 2)
        if live(i - 2):
            last_end(i - 2)
            gather_partner(i - 2)
        if live(i - 3):
            gather_relay(i - 3)
    for step in range(STEPS):
        if step >= STEPS - 2:
            exchange_sent(step)
            ring_sent(step, 1)
        ring_sent(step, 2)
        last_sent(step)
        gather_sent(step)
    router_sent()


def on_device(
    acts,
    grad_keys,
    grad_values,
    grad_logits,
    order,
    bucket_param,
    bucket_m,
    bucket_v,
    router_param,
    router_m,
    router_v,
):
    tree = scratch()
    names = tuple(tree)
    hbm = pl.BlockSpec(memory_space=pltpu.HBM)
    grad, router_grad = pl.pallas_call(
        lambda *refs: kernel(names, *refs),
        out_shape=(
            jax.ShapeDtypeStruct((BUCKETS, 2, 4, 16, 1024), F32),
            jax.ShapeDtypeStruct((1, 2048), F32),
        ),
        in_specs=[
            pl.BlockSpec(memory_space=pltpu.SMEM),
            pl.BlockSpec(memory_space=pltpu.VMEM),
            hbm,
            hbm,
            hbm,
        ],
        out_specs=(hbm, pl.BlockSpec(memory_space=pltpu.VMEM)),
        scratch_shapes=list(tree.values()),
        compiler_params=pltpu.CompilerParams(
            collective_id=0, has_side_effects=True, vmem_limit_bytes=58 * 1024 * 1024
        ),
        cost_estimate=pl.CostEstimate(flops=17_200_000_000, bytes_accessed=16_000_000, transcendentals=0),
        name="reduce",
    )(order, grad_logits, acts, grad_keys, grad_values)
    fresh = adamw(grad.reshape(bucket_param.shape), bucket_param, bucket_m, bucket_v)
    router_fresh = adamw(router_grad.reshape(router_param.shape), router_param, router_m, router_v)
    return fresh + router_fresh


def solution(mesh):
    state, router = P(None, "inst", None), P("inst", None)
    tokens = P(("rep", "inst"), None)
    return jax.shard_map(
        on_device,
        mesh=mesh,
        in_specs=(tokens, tokens, tokens, P(None, ("rep", "inst")), P(), state, state, state, router, router, router),
        out_specs=(state, state, state, router, router, router),
        check_vma=False,
    )
```

time: 603 us -> 143 us (0.24); the launches traced: 593 us -> 143 us
  waiting for transfers between devices: 298 us -> 0 us
  Pallas kernels: 0 us -> 134 us
  matrix products: 114 us -> 0 us
  between operations: 95.7 us -> 0.74 us
  blocking collectives: 27 us -> 0 us
  starting transfers between devices: 19.5 us -> 0 us
  local copies, waits for them, and re-layouts: 18.3 us -> 0.55 us
  other arithmetic: 21 us -> 7.68 us
    reduce_scatter x4 -> x0, waiting for transfers between devices: 241 us -> none  [owner_step(): share = lax.psum_scatter(term, 'inst', scatter_dimension=0, tiled=True)]
    pallas_call x0 -> x1, Pallas kernels: none -> 134 us  [on_device(): pl.pallas_call(lambda *refs: kernel(names, *refs), out_shape=(jax.ShapeDt...]
    dot_general x33 -> x0, matrix products: 114 us -> none  [the longest x32 108 us: contract(): lax.dot_general(left, right, (((0,), (0,)), ((), ())), preferred_element_...]
    all_to_all x4 -> x0, waiting for transfers between devices: 57.3 us -> none  [copy_for_each(): return lax.all_to_all(copies, axis, split_axis=0, concat_axis=0, tiled=True)]
    all_to_all x2 -> x0, blocking collectives: 27 us -> none  [the longest x1 15.2 us: sent_and_summed(): lax.all_to_all(split_up(shard, dim, devices), axis, 0, 0, tiled=True)]
    all_to_all x4 -> x0, starting transfers between devices: 18.7 us -> none  [copy_for_each(): return lax.all_to_all(copies, axis, split_axis=0, concat_axis=0, tiled=True)]
    broadcast_in_dim x5 -> x0, local copies, waits for them, and re-layouts: 14.2 us -> none  [copy_for_each(): copies = jnp.broadcast_to(shard, (lax.axis_size(axis), *shard.shape))]
    reduce_sum x6 -> x0, other arithmetic: 12.1 us -> none  [the longest x5 12.1 us: over_copies(): return jnp.sum(everything, axis=0)]
  transfers between devices with their start and end apart: 8 -> 0, of which waited for: 5 -> 0; matrix products, arithmetic and copies ran while one was open for 18% -> 0% of each run, Pallas kernels for 0% -> 0%
where the time goes in v1:
time: 143 us
  Pallas kernels  134 us (94%)
  other arithmetic  7.68 us (5%)
    pallas_call x1, Pallas kernels, on_device(): pl.pallas_call(lambda *refs: kernel(names, *refs), out_shape=(jax.ShapeDt...  134 us
    sub x2, other arithmetic, adamw(): param_new = param - step_rate * (ratio + decay_rate * param)  7.01 us

profile of v1, /device:TPU:0, one launch (start us, length us, event | category | flops | bytes accessed | tf_op | source)
XLA Modules:
  0.0 142.6 jit_solution(5226976102771747130)
XLA Ops:
  0.6 0.0 copy-start
  0.6 0.0 copy-start.1
  0.7 133.6 %reduce.5 = (f32[4,2,4,16,1024]{4,3,2,1,0:T(8,128)}, f32[1,2048]{1,0:T(1,128)}) custom-call(s32[32]{0:T(128)} %refs_0_.1, bf16[8,1024]{1,0:T(8,128)(2,1)} %refs_1_.1, bf16[1024,4096]{1,0:T(8,128)(2,1)} %refs_2_.1, bf16[1024,1024]{1,0:T(8,128)(2,1)} %refs_3_.1, bf16[1024,1024]{1,0:T(8,128)(2,1)} %refs_4_.1), custom_call_target="tpu_custom_call" | custom-call | flops 17200001024 | bytes 16000000 | tf_op jit(solution)/shard_map/reduce/pallas_call | solution.py:432
  134.3 0.0 copy-done
  134.3 0.0 copy-done.1
  134.3 0.0 copy-start.5
  134.3 0.0 copy-start.2
  134.3 0.0 copy-start.3
  134.4 0.0 copy-start.4
  134.4 6.4 %multiply_subtract_fusion = (f32[4,128,1024]{2,1,0:T(8,128)}, f32[4,128,1024]{2,1,0:T(8,128)}, f32[4,128,1024]{2,1,0:T(8,128)}) fusion(f32[4,128,1024]{2,1,0:T(8,128)S(1)} %copy-done, f32[4,2,4,16,1024]{4,3,2,1,0:T(8,128)} %get-tuple-element.8, f32[4,128,1024]{2,1,0:T(8,128)S(1)} %copy-done.1, f32[4,128,1024]{2,1,0:T(8,128)} %param.18), kind=kLoop, calls=%fused_computation.4 | loop fusion | flops 7864320 | bytes 14680064 | tf_op jit(solution)/shard_map/sub | solution.py:33
  140.7 0.5 broadcast.31
  141.2 0.0 copy-done.5
  141.2 0.7 reduce.4
  141.9 0.0 copy-done.2
  141.9 0.0 copy-done.3
  142.0 0.0 copy-done.4
  142.0 0.6 multiply_subtract_fusion.1
  (1 shorter events, 0.0 us)
Async XLA Ops:
  0.6 133.7 %copy-start = (f32[4,128,1024]{2,1,0:T(8,128)S(1)}, f32[4,128,1024]{2,1,0:T(8,128)}, u32[]{:S(2)}) copy-start(f32[4,128,1024]{2,1,0:T(8,128)} %param.16) | copy-start | bytes 6291460
  0.6 133.7 %copy-start.1 = (f32[4,128,1024]{2,1,0:T(8,128)S(1)}, f32[4,128,1024]{2,1,0:T(8,128)}, u32[]{:S(2)}) copy-start(f32[4,128,1024]{2,1,0:T(8,128)} %param.17) | copy-start | bytes 6291460
  134.3 6.9 %copy-start.5 = (f32[1,2048]{1,0:T(1,128)S(1)}, f32[1,2048]{1,0:T(1,128)}, u32[]{:S(2)}) copy-start(f32[1,2048]{1,0:T(1,128)} %get-tuple-element.9) | copy-start | bytes 24580
  134.3 7.6 %copy-start.2 = (f32[2,1024]{1,0:T(2,128)S(1)}, f32[2,1024]{1,0:T(2,128)}, u32[]{:S(2)}) copy-start(f32[2,1024]{1,0:T(2,128)} %param.19) | copy-start | bytes 24580
  134.3 7.6 %copy-start.3 = (f32[2,1024]{1,0:T(2,128)S(1)}, f32[2,1024]{1,0:T(2,128)}, u32[]{:S(2)}) copy-start(f32[2,1024]{1,0:T(2,128)} %param.20) | copy-start | bytes 24580
  134.4 7.6 %copy-start.4 = (f32[2,1024]{1,0:T(2,128)S(1)}, f32[2,1024]{1,0:T(2,128)}, u32[]{:S(2)}) copy-start(f32[2,1024]{1,0:T(2,128)} %param.21) | copy-start | bytes 24580

commit v2 on v1

v2 whole, which is shorter than its diff:
```python
import jax
import jax.numpy as jnp
from jax import lax
from jax.experimental import pallas as pl
from jax.experimental.pallas import tpu as pltpu
from jax.sharding import PartitionSpec as P

BUCKETS = 4
BLOCK_ROWS = 256
STEPS = 8
HALF = 512

beta_first = 0.9
beta_second = 0.95
step_rate = 0.05
decay_rate = 0.1
epsilon = 1e-08
correct_first = 1.0 - 0.9**10
correct_second = 1.0 - 0.95**10

VMEM_LIMIT = 56 * 1024 * 1024
MESH = pl.DeviceIdType.MESH
F32 = jnp.float32

DIMS = (("x", "y", "z"), ("y", "z", "x"), ("z", "x", "y"))
PARTS = (((0, 0, 16, 0), (3, 0, 8, 16)), ((1, 0, 16, 0), (3, 8, 8, 16)), ((2, 0, 16, 0),))
ROWS = (24, 24, 16)
W = 128
OWN = 4
SENT = 2


def adamw(grad, param, moment, second):
    moment_new = beta_first * moment + (1.0 - beta_first) * grad
    second_new = beta_second * second + (1.0 - beta_second) * grad * grad
    ratio = moment_new / correct_first / (jnp.sqrt(second_new / correct_second) + epsilon)
    param_new = param - step_rate * (ratio + decay_rate * param)
    return (param_new, moment_new, second_new)


def scratch():
    tree = {
        "acts": pltpu.VMEM((16, 1024, BLOCK_ROWS), jnp.bfloat16),
        "grads": pltpu.VMEM((2, 1024, 1024), jnp.bfloat16),
        "turned": pltpu.VMEM((BLOCK_ROWS, 1024), jnp.bfloat16),
        "out": pltpu.VMEM((BUCKETS, 2, 2, 4, 16, HALF), F32),
        "rt": pltpu.VMEM((2, 4, 2, 1, 2048), F32),
        "rx": pltpu.VMEM((4, 2, 1, 2048), F32),
        "rxx": pltpu.VMEM((3, 2, 1, 2048), F32),
        "rxy": pltpu.VMEM((4, 1, 2048), F32),
        "rxz": pltpu.VMEM((4, 1, 2048), F32),
        "ry": pltpu.VMEM((2, 1, 2048), F32),
        "load_sem": pltpu.SemaphoreType.DMA((18,)),
        "state_sem": pltpu.SemaphoreType.DMA((3,)),
        "x_send": pltpu.SemaphoreType.DMA((STEPS, 3)),
        "x_recv": pltpu.SemaphoreType.DMA((STEPS, 3)),
        "p1_send": pltpu.SemaphoreType.DMA((STEPS, 3, 6)),
        "p1_recv": pltpu.SemaphoreType.DMA((STEPS, 3, 6)),
        "p2_send": pltpu.SemaphoreType.DMA((STEPS, 3, 6)),
        "p2_recv": pltpu.SemaphoreType.DMA((STEPS, 3, 6)),
        "p3_send": pltpu.SemaphoreType.DMA((STEPS, 3, 3)),
        "p3_recv": pltpu.SemaphoreType.DMA((STEPS, 3, 3)),
        "ag_send": pltpu.SemaphoreType.DMA((STEPS, 5)),
        "ag_recv": pltpu.SemaphoreType.DMA((STEPS, 5)),
        "r_send": pltpu.SemaphoreType.DMA((10,)),
        "r_recv": pltpu.SemaphoreType.DMA((10,)),
    }
    for q in range(3):
        r = ROWS[q]
        tree[f"own{q}"] = pltpu.VMEM((OWN, 4, 4, 4, r, W), F32)
        tree[f"sent{q}"] = pltpu.VMEM((SENT, 4, 4, 4, r, W), F32)
        tree[f"xr{q}"] = pltpu.VMEM((4, 4, 4, 4, r, W), F32)
        tree[f"ra{q}"] = pltpu.VMEM((4, 6, 2, 4, r, W), F32)
        tree[f"q{q}"] = pltpu.VMEM((STEPS, 4, 4, r, W), F32)
        tree[f"rb{q}"] = pltpu.VMEM((STEPS, 6, 2, r, W), F32)
        tree[f"rc{q}"] = pltpu.VMEM((STEPS, 3, r, W), F32)
    return tree


def kernel(names, order, logits, acts_hbm, keys_hbm, values_hbm, *refs):
    state_hbm, router_state = refs[0:3], refs[3:6]
    state, router_new = refs[6:9], refs[9:12]
    refs = refs[12:]
    ref = dict(zip(names, refs))
    rep = lax.axis_index("rep")
    inst = lax.axis_index("inst")
    yl, z = rep // 4, rep % 4
    yh, x, core = inst // 8, (inst // 2) % 4, inst % 2
    place = {"x": x, "y": yh * 2 + yl, "z": z, "c": core}

    def device(**change):
        at = {**place, **change}
        y = at["y"]
        return {"rep": (y % 2) * 4 + at["z"], "inst": ((y // 2) * 4 + at["x"]) * 2 + at["c"]}

    def along(dim, delta):
        return device(**{dim: (place[dim] + delta) % 4})

    sibling = device(c=1 - core)
    partner = device(y=yh * 2 + (1 - yl))

    def send(src, dst, send_sem, recv_sem, to):
        copy = pltpu.make_async_remote_copy(
            src_ref=src, dst_ref=dst, send_sem=send_sem, recv_sem=recv_sem, device_id=to, device_id_type=MESH
        )
        copy.start()

    def wait_recv(dst, sem):
        pltpu.make_async_copy(dst, dst, sem).wait()

    wait_send = wait_recv

    loads = [
        pltpu.make_async_copy(keys_hbm, ref["grads"].at[0], ref["load_sem"].at[16]),
        pltpu.make_async_copy(values_hbm, ref["grads"].at[1], ref["load_sem"].at[17]),
    ]
    for i in range(16):
        loads.append(
            pltpu.make_async_copy(
                acts_hbm.at[:, i * BLOCK_ROWS : (i + 1) * BLOCK_ROWS], ref["acts"].at[i], ref["load_sem"].at[i]
            )
        )
    for load in loads:
        load.start()
    state_loads = [pltpu.make_async_copy(state_hbm[n], state[n], ref["state_sem"].at[n]) for n in range(3)]

    barrier = pltpu.get_barrier_semaphore()
    peers = [sibling] + [along(d, delta) for d in "xyz" for delta in (1, 2, 3)]
    for peer in peers:
        pl.semaphore_signal(barrier, inc=1, device_id=peer, device_id_type=MESH)

    def router_term():
        for i in range(16):
            term = jnp.dot(logits[...], ref["acts"][i], preferred_element_type=F32)
            for e in range(8):
                ref["rt"][i // 8, e % 4, e // 4, :, pl.ds((i % 8) * 256, 256)] = term[e : e + 1, :]

    def spots(q, slot_y, slot_x):
        if q == 0:
            return (slot_x, pl.ds(slot_y * 2, 2))
        if q == 1:
            return (pl.ds(slot_y * 2, 2), pl.ds(0, 4), slot_x)
        return (pl.ds(0, 4), slot_x, pl.ds(slot_y * 2, 2))

    def exchange(step, j):
        for q in range(3):
            spot = spots(q, j // 4, j % 4)
            send(
                ref[f"sent{q}"].at[(step % SENT,) + spot],
                ref[f"xr{q}"].at[(step % 4,) + spot],
                ref["x_send"].at[step, q],
                ref["x_recv"].at[step, q],
                sibling,
            )

    def matmul(step, first, last):
        bucket, par = step // 2, step % 2

        def body(j, carry):
            slot_y, slot_x = j // 4, j % 4
            block = order[bucket * 8 + j]
            for h, side in enumerate((core, 1 - core)):
                columns = ref["acts"][block % 16, :, pl.ds(pl.multiple_of(side * 128, 128), 128)]
                ref["turned"][h * 128 : (h + 1) * 128] = columns.T
            for n in range(2):
                lo = n * 256
                piece = jnp.dot(
                    ref["turned"][...],
                    ref["grads"][block // 16, :, par * HALF + lo : par * HALF + lo + 256],
                    preferred_element_type=F32,
                )
                for h in range(2):
                    dst = "sent" if h else "own"
                    slot = step % (SENT if h else OWN)
                    for q in range(3):
                        for chunk, top, count, row in PARTS[q]:
                            if chunk // 2 != n:
                                continue
                            left = chunk % 2 * W
                            for l in range(2):
                                y = slot_y * 2 + l
                                for k in range(4):
                                    start = h * 128 + l * 64 + k * 16 + top
                                    value = piece[start : start + count, left : left + W]
                                    at = ((slot_x, y, k), (y, k, slot_x), (k, slot_x, y))[q]
                                    ref[f"{dst}{q}"][(slot,) + at + (pl.ds(row, count),)] = value

            @pl.when(j > first)
            def _():
                exchange(step, j - 1)

            return carry

        lax.fori_loop(first, last, body, 0)
        exchange(step, last - 1)

    def add_sibling(step):
        for q in range(3):
            own, xr = ref[f"own{q}"], ref[f"xr{q}"]
            wait_recv(xr.at[step % 4], ref["x_recv"].at[step, q])

            def body(d, carry):
                own[step % OWN, d] = own[step % OWN, d] + xr[step % 4, d]
                return carry

            lax.fori_loop(0, 4, body, 0)

    def views(step, q, phase):
        slot = step % OWN if phase == 1 else step
        src, recv = (ref[f"own{q}"], ref[f"ra{q}"]) if phase == 1 else (ref[f"q{q}"], ref[f"rb{q}"])
        return src, (lambda d, h: (slot, d, pl.ds(2 * h, 2))), recv, (step % 4 if phase == 1 else step)

    def ring_send(step, q, phase, m, where, delta):
        src, at, recv, b = views(step, q, phase)
        dim = DIMS[q][phase - 1]
        d, h = where
        send(
            src.at[at((place[dim] + d) % 4, h)],
            recv.at[b, m],
            ref[f"p{phase}_send"].at[step, q, m],
            ref[f"p{phase}_recv"].at[step, q, m],
            along(dim, delta),
        )

    def ring_start(step, phase):
        for q in range(3):
            ring_send(step, q, phase, 0, (2, 0), 1)
            ring_send(step, q, phase, 1, (2, 1), 3)
            ring_send(step, q, phase, 2, (1, 1), 1)
            ring_send(step, q, phase, 3, (3, 0), 3)

    def ring_relay(step, phase):
        for q in range(3):
            src, at, recv, b = views(step, q, phase)
            here = place[DIMS[q][phase - 1]]
            for m, d, h in ((0, 1, 0), (1, 3, 1)):
                wait_recv(recv.at[b, m], ref[f"p{phase}_recv"].at[step, q, m])
                spot = at((here + d) % 4, h)
                src[spot] = src[spot] + recv[b, m]
                ring_send(step, q, phase, 4 + m, (d, h), d)

    def ring_end(step, phase):
        for q in range(3):
            src, at, recv, b = views(step, q, phase)
            here = place[DIMS[q][phase - 1]]
            for h, arrived in ((0, (3, 4)), (1, (2, 5))):
                for m in arrived:
                    wait_recv(recv.at[b, m], ref[f"p{phase}_recv"].at[step, q, m])
                spot = at(here, h)
                total = src[spot] + recv[b, arrived[0]] + recv[b, arrived[1]]
                if phase == 1:
                    ref[f"q{q}"][step, pl.ds(2 * h, 2)] = total
                else:
                    src[spot] = total

    def ring_sent(step, phase):
        for q in range(3):
            _, _, recv, b = views(step, q, phase)
            for m in range(6):
                wait_send(recv.at[b, m], ref[f"p{phase}_send"].at[step, q, m])

    def exchange_sent(step):
        for q in range(3):
            wait_send(ref[f"xr{q}"].at[step % 4], ref["x_send"].at[step, q])

    def last_start(step):
        for q in range(3):
            second, third = DIMS[q][1:]
            for m in range(3):
                delta = (1, 3, 2)[m]
                send(
                    ref[f"q{q}"].at[step, place[second], (place[third] + delta) % 4],
                    ref[f"rc{q}"].at[step, m],
                    ref["p3_send"].at[step, q, m],
                    ref["p3_recv"].at[step, q, m],
                    along(third, delta),
                )

    def last_end(step):
        b, par = step // 2, step % 2
        for q in range(3):
            second, third = DIMS[q][1:]
            rc = ref[f"rc{q}"]
            for m in range(3):
                wait_recv(rc.at[step, m], ref["p3_recv"].at[step, q, m])
            total = ref[f"q{q}"][step, place[second], place[third]] + rc[step, 0] + rc[step, 1] + rc[step, 2]
            for chunk, top, count, row in PARTS[q]:
                ref["out"][b, par, yl, z, pl.ds(top, count), pl.ds(chunk * W, W)] = total[row : row + count]

    def last_sent(step):
        for q in range(3):
            for m in range(3):
                wait_send(ref[f"rc{q}"].at[step, m], ref["p3_send"].at[step, q, m])

    def gather_send(step, n, spot, to):
        out = ref["out"].at[(step // 2, step % 2) + spot]
        send(out, out, ref["ag_send"].at[step, n], ref["ag_recv"].at[step, n], to)

    def gather_wait(step, n, spot, which="ag_recv"):
        wait_recv(ref["out"].at[(step // 2, step % 2) + spot], ref[which].at[step, n])

    both = pl.ds(0, 2)

    def gather_partner(step):
        gather_send(step, 0, (yl, z), partner)

    def gather_start(step):
        gather_wait(step, 0, (1 - yl, z))
        gather_send(step, 1, (both, z), along("z", 1))
        gather_send(step, 2, (both, z), along("z", 3))

    def gather_relay(step):
        gather_wait(step, 1, (both, (z + 3) % 4))
        gather_send(step, 3, (0, (z + 3) % 4), along("z", 1))
        gather_wait(step, 2, (both, (z + 1) % 4))
        gather_send(step, 4, (1, (z + 1) % 4), along("z", 3))

    def gather_end(step):
        gather_wait(step, 3, (0, (z + 2) % 4))
        gather_wait(step, 4, (1, (z + 2) % 4))
        b, par = step // 2, step % 2
        columns = pl.ds(par * HALF, HALF)

        def body(i, carry):
            rows = pl.ds(pl.multiple_of(i * 16, 16), 16)
            grad = ref["out"][b, par, i // 4, i % 4]
            fresh = adamw(grad, *(part[b, rows, columns] for part in state))
            for part, value in zip(state, fresh):
                part[b, rows, columns] = value
            return carry

        lax.fori_loop(0, 8, body, 0)

    def gather_sent(step):
        for n, spot in enumerate(((yl, z), (both, z), (both, z), (0, z), (1, z))):
            gather_wait(step, n, spot, "ag_send")

    def state_start():
        for load in state_loads:
            load.start()

    def state_end():
        for load in state_loads:
            load.wait()

    def router_send(n, src, dst, to):
        send(src, dst, ref["r_send"].at[n], ref["r_recv"].at[n], to)

    def router_wait(n, dst):
        wait_recv(dst, ref["r_recv"].at[n])

    def router_0():
        router_send(0, ref["rt"].at[1 - core], ref["rx"], sibling)

    def router_1():
        router_wait(0, ref["rx"])
        ref["rt"][core] = ref["rt"][core] + ref["rx"][...]
        for m, delta in enumerate((1, 2, 3)):
            router_send(1 + m, ref["rt"].at[core, (x + delta) % 4], ref["rxx"].at[m], along("x", delta))

    def router_2():
        for m in range(3):
            router_wait(1 + m, ref["rxx"].at[m])
        ref["ry"][...] = ref["rt"][core, x] + ref["rxx"][0] + ref["rxx"][1] + ref["rxx"][2]
        here = place["y"]
        ref["rxy"][here] = ref["ry"][yh]
        for m, delta in enumerate((1, 2, 3)):
            to = (here + delta) % 4
            router_send(4 + m, ref["ry"].at[to // 2], ref["rxy"].at[here], along("y", delta))

    def router_3():
        here = place["y"]
        for m, delta in enumerate((1, 2, 3)):
            router_wait(4 + m, ref["rxy"].at[(here - delta) % 4])
        total = ref["rxy"][0] + ref["rxy"][1] + ref["rxy"][2] + ref["rxy"][3]
        ref["rxz"][z] = total
        for m, delta in enumerate((1, 2, 3)):
            router_send(7 + m, ref["rxz"].at[z], ref["rxz"].at[z], along("z", delta))

    def router_4():
        for m, delta in enumerate((1, 2, 3)):
            router_wait(7 + m, ref["rxz"].at[(z - delta) % 4])
        total = ref["rxz"][0] + ref["rxz"][1] + ref["rxz"][2] + ref["rxz"][3]
        for row in range(2):
            at = pl.ds(row, 1)
            fresh = adamw(total[:, row * 1024 : (row + 1) * 1024], *(part[at] for part in router_state))
            for part, value in zip(router_new, fresh):
                part[at] = value

    def router_sent():
        wait_send(ref["rx"], ref["r_send"].at[0])
        for m in range(3):
            wait_send(ref["rxx"].at[m], ref["r_send"].at[1 + m])
            wait_send(ref["rxy"].at[m], ref["r_send"].at[4 + m])
            wait_send(ref["rxz"].at[m], ref["r_send"].at[7 + m])

    router_stages = {0: router_0, 1: router_1, 2: router_2, 3: router_3, 4: router_4}

    def run(stage, *args):
        with jax.named_scope(f"{stage.__name__}#s={'_'.join(map(str, args))}"):
            stage(*args)

    def live(step):
        return 0 <= step < STEPS

    with jax.named_scope("loads"):
        for load in loads:
            load.wait()
    with jax.named_scope("barrier"):
        pl.semaphore_wait(barrier, len(peers))
    run(matmul, 0, 0, 8)
    run(router_term)
    state_start()
    run(router_0)
    run(add_sibling, 0)
    run(ring_start, 0, 1)
    run(matmul, 1, 0, 8)
    for i in range(STEPS + 4):
        if live(i + 2):
            if live(i):
                run(exchange_sent, i)
            if live(i - 2):
                run(ring_sent, i - 2, 1)
            run(matmul, i + 2, 0, 4)
        if live(i - 2):
            run(ring_end, i - 2, 2)
            run(last_start, i - 2)
        if live(i - 1):
            run(ring_end, i - 1, 1)
            run(ring_start, i - 1, 2)
        if live(i - 3):
            run(gather_start, i - 3)
        if live(i + 2):
            run(matmul, i + 2, 4, 8)
        if live(i):
            run(ring_relay, i, 1)
        if live(i + 1):
            run(add_sibling, i + 1)
            run(ring_start, i + 1, 1)
        if live(i - 1):
            run(ring_relay, i - 1, 2)
        if live(i - 2):
            run(last_end, i - 2)
            run(gather_partner, i - 2)
        if live(i - 3):
            run(gather_relay, i - 3)
        if i + 1 in router_stages:
            run(router_stages[i + 1])
        if live(i - 4):
            if i == 4:
                run(state_end)
            run(gather_end, i - 4)
    with jax.named_scope("ending"):
        for step in range(STEPS):
            if step >= STEPS - 2:
                exchange_sent(step)
            if step >= STEPS - 4:
                ring_sent(step, 1)
            ring_sent(step, 2)
            last_sent(step)
            gather_sent(step)
        router_sent()


def on_device(
    acts,
    grad_keys,
    grad_values,
    grad_logits,
    order,
    bucket_param,
    bucket_m,
    bucket_v,
    router_param,
    router_m,
    router_v,
):
    tree = scratch()
    names = tuple(tree)
    hbm, vmem = pl.BlockSpec(memory_space=pltpu.HBM), pl.BlockSpec(memory_space=pltpu.VMEM)
    return pl.pallas_call(
        lambda *refs: kernel(names, *refs),
        out_shape=tuple(
            pltpu.VMEM(part.shape, F32) for part in (bucket_param, bucket_m, bucket_v, router_param, router_m, router_v)
        ),
        in_specs=[pl.BlockSpec(memory_space=pltpu.SMEM), vmem] + [hbm] * 6 + [vmem] * 3,
        out_specs=(vmem,) * 6,
        scratch_shapes=list(tree.values()),
        compiler_params=pltpu.CompilerParams(
            collective_id=0, has_side_effects=True, vmem_limit_bytes=VMEM_LIMIT
        ),
        cost_estimate=pl.CostEstimate(flops=17_200_000_000, bytes_accessed=24_000_000, transcendentals=0),
        name="reduce",
    )(
        order,
        grad_logits,
        acts,
        grad_keys,
        grad_values,
        bucket_param,
        bucket_m,
        bucket_v,
        router_param,
        router_m,
        router_v,
    )


def solution(mesh):
    state, router = P(None, "inst", None), P("inst", None)
    tokens = P(("rep", "inst"), None)
    return jax.shard_map(
        on_device,
        mesh=mesh,
        in_specs=(tokens, tokens, tokens, P(None, ("rep", "inst")), P(), state, state, state, router, router, router),
        out_specs=(state, state, state, router, router, router),
        check_vma=False,
    )
```

time: 143 us -> 138 us (0.965)
  other arithmetic: 7.68 us -> 0 us
  local copies, waits for them, and re-layouts: 0.55 us -> 5.75 us
  Pallas kernels: 134 us -> 131 us
    sub x2 -> x0, other arithmetic: 7.01 us -> none  [adamw(): param_new = param - step_rate * (ratio + decay_rate * param)]
    unnamed x12 -> x6, local copies, waits for them, and re-layouts: 0.03 us -> 5.75 us
    pallas_call x1, Pallas kernels: 134 us -> 131 us  [on_device(): pl.pallas_call(lambda *refs: kernel(names, *refs), out_shape=tuple((pltpu...]
where the time goes in v2:
time: 138 us
  Pallas kernels  131 us (95%)
  local copies, waits for them, and re-layouts  5.75 us (4%)
    pallas_call x1, Pallas kernels, on_device(): pl.pallas_call(lambda *refs: kernel(names, *refs), out_shape=tuple((pltpu...  131 us
    unnamed x6, local copies, waits for them, and re-layouts  5.75 us

profile of v2, /device:TPU:0, one launch (start us, length us, event | category | flops | bytes accessed | tf_op | source)
XLA Modules:
  0.0 137.6 jit_solution(5863790379516709206)
XLA Ops:
  0.6 131.2 %reduce.1 = (f32[4,128,1024]{2,1,0:T(8,128)S(1)}, f32[4,128,1024]{2,1,0:T(8,128)S(1)}, f32[4,128,1024]{2,1,0:T(8,128)S(1)}, f32[2,1024]{1,0:T(2,128)S(1)}, f32[2,1024]{1,0:T(2,128)S(1)}, /*index=5*/f32[2,1024]{1,0:T(2,128)S(1)}) custom-call(s32[32]{0:T(128)} %refs_0_.1, bf16[8,1024]{1,0:T(8,128)(2,1)} %refs_1_.1, bf16[1024,4096]{1,0:T(8,128)(2,1)} %refs_2_.1, ...), custom_call_target="tpu_custom_call" | custom-call | flops 17200001024 | bytes 24000000 | tf_op jit(solution)/shard_map/reduce/pallas_call | solution.py:481
  131.9 1.3 copy.23
  133.2 0.6 copy.26
  133.8 0.6 copy.27
  134.4 0.6 copy.28
  135.0 1.3 copy.24
  136.3 1.3 copy.25

commit v3 on v2

--- a/solution.py
+++ b/solution.py
@@ -22,12 +22,13 @@
 MESH = pl.DeviceIdType.MESH
 F32 = jnp.float32
 
-DIMS = (("x", "y", "z"), ("y", "z", "x"), ("z", "x", "y"))
+DIMS = (("x", "z", "y"), ("y", "x", "z"), ("z", "y", "x"))
 PARTS = (((0, 0, 16, 0), (3, 0, 8, 16)), ((1, 0, 16, 0), (3, 8, 8, 16)), ((2, 0, 16, 0),))
 ROWS = (24, 24, 16)
 W = 128
 OWN = 4
 SENT = 2
+DIRECT = (STEPS - 1,)
 
 
 def adamw(grad, param, moment, second):
@@ -41,7 +42,8 @@
 def scratch():
     tree = {
         "acts": pltpu.VMEM((16, 1024, BLOCK_ROWS), jnp.bfloat16),
-        "grads": pltpu.VMEM((2, 1024, 1024), jnp.bfloat16),
+        "grads0": pltpu.VMEM((2, 1024, HALF), jnp.bfloat16),
+        "grads1": pltpu.VMEM((2, 1024, HALF), jnp.bfloat16),
         "turned": pltpu.VMEM((BLOCK_ROWS, 1024), jnp.bfloat16),
         "out": pltpu.VMEM((BUCKETS, 2, 2, 4, 16, HALF), F32),
         "rt": pltpu.VMEM((2, 4, 2, 1, 2048), F32),
@@ -50,7 +52,7 @@
         "rxy": pltpu.VMEM((4, 1, 2048), F32),
         "rxz": pltpu.VMEM((4, 1, 2048), F32),
         "ry": pltpu.VMEM((2, 1, 2048), F32),
-        "load_sem": pltpu.SemaphoreType.DMA((18,)),
+        "load_sem": pltpu.SemaphoreType.DMA((20,)),
         "state_sem": pltpu.SemaphoreType.DMA((3,)),
         "x_send": pltpu.SemaphoreType.DMA((STEPS, 3)),
         "x_recv": pltpu.SemaphoreType.DMA((STEPS, 3)),
@@ -62,6 +64,8 @@
         "p3_recv": pltpu.SemaphoreType.DMA((STEPS, 3, 3)),
         "ag_send": pltpu.SemaphoreType.DMA((STEPS, 5)),
         "ag_recv": pltpu.SemaphoreType.DMA((STEPS, 5)),
+        "d_send": pltpu.SemaphoreType.DMA((STEPS, 7)),
+        "d_recv": pltpu.SemaphoreType.DMA((STEPS, 7)),
         "r_send": pltpu.SemaphoreType.DMA((10,)),
         "r_recv": pltpu.SemaphoreType.DMA((10,)),
     }
@@ -72,7 +76,7 @@
         tree[f"xr{q}"] = pltpu.VMEM((4, 4, 4, 4, r, W), F32)
         tree[f"ra{q}"] = pltpu.VMEM((4, 6, 2, 4, r, W), F32)
         tree[f"q{q}"] = pltpu.VMEM((STEPS, 4, 4, r, W), F32)
-        tree[f"rb{q}"] = pltpu.VMEM((STEPS, 6, 2, r, W), F32)
+        tree[f"rb{q}"] = pltpu.VMEM((STEPS, 12, r, W), F32)
         tree[f"rc{q}"] = pltpu.VMEM((STEPS, 3, r, W), F32)
     return tree
 
@@ -110,17 +114,25 @@
 
     wait_send = wait_recv
 
-    loads = [
-        pltpu.make_async_copy(keys_hbm, ref["grads"].at[0], ref["load_sem"].at[16]),
-        pltpu.make_async_copy(values_hbm, ref["grads"].at[1], ref["load_sem"].at[17]),
-    ]
+    def grad_loads(half):
+        return [
+            pltpu.make_async_copy(
+                part.at[:, half * HALF : (half + 1) * HALF],
+                ref[f"grads{half}"].at[n],
+                ref["load_sem"].at[16 + half * 2 + n],
+            )
+            for n, part in enumerate((keys_hbm, values_hbm))
+        ]
+
+    loads = grad_loads(0)
     for i in range(16):
         loads.append(
             pltpu.make_async_copy(
                 acts_hbm.at[:, i * BLOCK_ROWS : (i + 1) * BLOCK_ROWS], ref["acts"].at[i], ref["load_sem"].at[i]
             )
         )
-    for load in loads:
+    late_loads = grad_loads(1)
+    for load in loads + late_loads:
         load.start()
     state_loads = [pltpu.make_async_copy(state_hbm[n], state[n], ref["state_sem"].at[n]) for n in range(3)]
 
@@ -136,11 +148,8 @@
                 ref["rt"][i // 8, e % 4, e // 4, :, pl.ds((i % 8) * 256, 256)] = term[e : e + 1, :]
 
     def spots(q, slot_y, slot_x):
-        if q == 0:
-            return (slot_x, pl.ds(slot_y * 2, 2))
-        if q == 1:
-            return (pl.ds(slot_y * 2, 2), pl.ds(0, 4), slot_x)
-        return (pl.ds(0, 4), slot_x, pl.ds(slot_y * 2, 2))
+        pair, every = pl.ds(slot_y * 2, 2), pl.ds(0, 4)
+        return ((slot_x, every, pair), (pair, slot_x, every), (every, pair, slot_x))[q]
 
     def exchange(step, j):
         for q in range(3):
@@ -166,7 +175,7 @@
                 lo = n * 256
                 piece = jnp.dot(
                     ref["turned"][...],
-                    ref["grads"][block // 16, :, par * HALF + lo : par * HALF + lo + 256],
+                    ref[f"grads{par}"][block // 16, :, lo : lo + 256],
                     preferred_element_type=F32,
                 )
                 for h in range(2):
@@ -182,7 +191,7 @@
                                 for k in range(4):
                                     start = h * 128 + l * 64 + k * 16 + top
                                     value = piece[start : start + count, left : left + W]
-                                    at = ((slot_x, y, k), (y, k, slot_x), (k, slot_x, y))[q]
+                                    at = ((slot_x, k, y), (y, slot_x, k), (k, y, slot_x))[q]
                                     ref[f"{dst}{q}"][(slot,) + at + (pl.ds(row, count),)] = value
 
             @pl.when(j > first)
@@ -208,15 +217,17 @@
     def views(step, q, phase):
         slot = step % OWN if phase == 1 else step
         src, recv = (ref[f"own{q}"], ref[f"ra{q}"]) if phase == 1 else (ref[f"q{q}"], ref[f"rb{q}"])
-        return src, (lambda d, h: (slot, d, pl.ds(2 * h, 2))), recv, (step % 4 if phase == 1 else step)
+        at = lambda d, h: (slot, d, pl.ds(2 * h, 2))
+        into = (lambda m: (step % 4, m)) if phase == 1 else (lambda m: (step, pl.ds(2 * m, 2)))
+        return src, at, recv, into
 
     def ring_send(step, q, phase, m, where, delta):
-        src, at, recv, b = views(step, q, phase)
+        src, at, recv, into = views(step, q, phase)
         dim = DIMS[q][phase - 1]
         d, h = where
         send(
             src.at[at((place[dim] + d) % 4, h)],
-            recv.at[b, m],
+            recv.at[into(m)],
             ref[f"p{phase}_send"].at[step, q, m],
             ref[f"p{phase}_recv"].at[step, q, m],
             along(dim, delta),
@@ -226,28 +237,31 @@
         for q in range(3):
             ring_send(step, q, phase, 0, (2, 0), 1)
             ring_send(step, q, phase, 1, (2, 1), 3)
+
+    def ring_next(step, phase):
+        for q in range(3):
             ring_send(step, q, phase, 2, (1, 1), 1)
             ring_send(step, q, phase, 3, (3, 0), 3)
 
     def ring_relay(step, phase):
         for q in range(3):
-            src, at, recv, b = views(step, q, phase)
+            src, at, recv, into = views(step, q, phase)
             here = place[DIMS[q][phase - 1]]
             for m, d, h in ((0, 1, 0), (1, 3, 1)):
-                wait_recv(recv.at[b, m], ref[f"p{phase}_recv"].at[step, q, m])
+                wait_recv(recv.at[into(m)], ref[f"p{phase}_recv"].at[step, q, m])
                 spot = at((here + d) % 4, h)
-                src[spot] = src[spot] + recv[b, m]
+                src[spot] = src[spot] + recv[into(m)]
                 ring_send(step, q, phase, 4 + m, (d, h), d)
 
     def ring_end(step, phase):
         for q in range(3):
-            src, at, recv, b = views(step, q, phase)
+            src, at, recv, into = views(step, q, phase)
             here = place[DIMS[q][phase - 1]]
             for h, arrived in ((0, (3, 4)), (1, (2, 5))):
                 for m in arrived:
-                    wait_recv(recv.at[b, m], ref[f"p{phase}_recv"].at[step, q, m])
+                    wait_recv(recv.at[into(m)], ref[f"p{phase}_recv"].at[step, q, m])
                 spot = at(here, h)
-                total = src[spot] + recv[b, arrived[0]] + recv[b, arrived[1]]
+                total = src[spot] + recv[into(arrived[0])] + recv[into(arrived[1])]
                 if phase == 1:
                     ref[f"q{q}"][step, pl.ds(2 * h, 2)] = total
                 else:
@@ -255,9 +269,36 @@
 
     def ring_sent(step, phase):
         for q in range(3):
-            _, _, recv, b = views(step, q, phase)
+            _, _, recv, into = views(step, q, phase)
             for m in range(6):
-                wait_send(recv.at[b, m], ref[f"p{phase}_send"].at[step, q, m])
+                wait_send(recv.at[into(m)], ref[f"p{phase}_send"].at[step, q, m])
+
+    def second_start(step):
+        for m, delta in enumerate((2, 1, 3)):
+            for q in range(3):
+                dim = DIMS[q][1]
+                send(
+                    ref[f"q{q}"].at[step, (place[dim] + delta) % 4],
+                    ref[f"rb{q}"].at[step, pl.ds(4 * m, 4)],
+                    ref["p2_send"].at[step, q, m],
+                    ref["p2_recv"].at[step, q, m],
+                    along(dim, delta),
+                )
+
+    def second_end(step):
+        for q in range(3):
+            rb, here = ref[f"rb{q}"], place[DIMS[q][1]]
+            for m in range(3):
+                wait_recv(rb.at[step, pl.ds(4 * m, 4)], ref["p2_recv"].at[step, q, m])
+            total = ref[f"q{q}"][step, here]
+            for m in range(3):
+                total = total + rb[step, pl.ds(4 * m, 4)]
+            ref[f"q{q}"][step, here] = total
+
+    def second_sent(step):
+        for q in range(3):
+            for m in range(3):
+                wait_send(ref[f"rb{q}"].at[step, pl.ds(4 * m, 4)], ref["p2_send"].at[step, q, m])
 
     def exchange_sent(step):
         for q in range(3):
@@ -315,9 +356,23 @@
         gather_wait(step, 2, (both, (z + 1) % 4))
         gather_send(step, 4, (1, (z + 1) % 4), along("z", 3))
 
+    def gather_direct(step):
+        b, par = step // 2, step % 2
+        own = ref["out"].at[b, par, yl, z]
+        for n in (5, 1, 6, 2, 4, 0, 3):
+            dy, dz = divmod(n + 1, 4)
+            to = device(y=yh * 2 + (yl + dy) % 2, z=(z + dz) % 4)
+            send(own, own, ref["d_send"].at[step, n], ref["d_recv"].at[step, n], to)
+
     def gather_end(step):
-        gather_wait(step, 3, (0, (z + 2) % 4))
-        gather_wait(step, 4, (1, (z + 2) % 4))
+        if step in DIRECT:
+            for n in range(7):
+                dy, dz = divmod(n + 1, 4)
+                there = ref["out"].at[step // 2, step % 2, (yl + dy) % 2, (z - dz) % 4]
+                wait_recv(there, ref["d_recv"].at[step, n])
+        else:
+            gather_wait(step, 3, (0, (z + 2) % 4))
+            gather_wait(step, 4, (1, (z + 2) % 4))
         b, par = step // 2, step % 2
         columns = pl.ds(par * HALF, HALF)
 
@@ -332,6 +387,10 @@
         lax.fori_loop(0, 8, body, 0)
 
     def gather_sent(step):
+        if step in DIRECT:
+            for n in range(7):
+                wait_send(ref["out"].at[step // 2, step % 2, yl, z], ref["d_send"].at[step, n])
+            return
         for n, spot in enumerate(((yl, z), (both, z), (both, z), (0, z), (1, z))):
             gather_wait(step, n, spot, "ag_send")
 
@@ -410,55 +469,76 @@
         pl.semaphore_wait(barrier, len(peers))
     run(matmul, 0, 0, 8)
     run(router_term)
-    state_start()
     run(router_0)
     run(add_sibling, 0)
     run(ring_start, 0, 1)
-    run(matmul, 1, 0, 8)
-    for i in range(STEPS + 4):
-        if live(i + 2):
-            if live(i):
-                run(exchange_sent, i)
-            if live(i - 2):
-                run(ring_sent, i - 2, 1)
-            run(matmul, i + 2, 0, 4)
-        if live(i - 2):
-            run(ring_end, i - 2, 2)
-            run(last_start, i - 2)
+    for load in late_loads:
+        load.wait()
+    state_start()
+
+    def all_sent(step):
+        if step in DIRECT:
+            second_sent(step)
+        else:
+            ring_sent(step, 2)
+        last_sent(step)
+        gather_sent(step)
+
+    for i in range(STEPS + 5):
+        if live(i - 2) and i - 2 not in DIRECT:
+            run(ring_relay, i - 2, 2)
+        if live(i):
+            run(ring_next, i, 1)
+        if live(i + 1):
+            if live(i - 1):
+                run(exchange_sent, i - 1)
+            if live(i - 3):
+                run(ring_sent, i - 3, 1)
+            run(matmul, i + 1, 0, 4)
         if live(i - 1):
             run(ring_end, i - 1, 1)
-            run(ring_start, i - 1, 2)
-        if live(i - 3):
-            run(gather_start, i - 3)
-        if live(i + 2):
-            run(matmul, i + 2, 4, 8)
+            if i - 1 in DIRECT:
+                run(second_start, i - 1)
+            else:
+                run(ring_start, i - 1, 2)
+                run(ring_next, i - 1, 2)
+        if live(i + 1):
+            run(matmul, i + 1, 4, 8)
         if live(i):
             run(ring_relay, i, 1)
+        if live(i - 2):
+            if i - 2 in DIRECT:
+                run(second_end, i - 2)
+            else:
+                run(ring_end, i - 2, 2)
+            run(last_start, i - 2)
         if live(i + 1):
             run(add_sibling, i + 1)
             run(ring_start, i + 1, 1)
-        if live(i - 1):
-            run(ring_relay, i - 1, 2)
-        if live(i - 2):
-            run(last_end, i - 2)
-            run(gather_partner, i - 2)
         if live(i - 3):
-            run(gather_relay, i - 3)
+            run(last_end, i - 3)
+            if i - 3 in DIRECT:
+                run(gather_direct, i - 3)
+            else:
+                run(gather_partner, i - 3)
+        if live(i - 4) and i - 4 not in DIRECT:
+            run(gather_start, i - 4)
+        if live(i - 5) and i - 5 not in DIRECT:
+            run(gather_relay, i - 5)
         if i + 1 in router_stages:
             run(router_stages[i + 1])
-        if live(i - 4):
-            if i == 4:
-                run(state_end)
-            run(gather_end, i - 4)
+        if i == 5:
+            run(state_end)
+        if live(i - 6):
+            run(gather_end, i - 6)
+            run(all_sent, i - 6)
+    run(gather_end, STEPS - 1)
     with jax.named_scope("ending"):
-        for step in range(STEPS):
+        for step in range(STEPS - 4, STEPS):
             if step >= STEPS - 2:
                 exchange_sent(step)
-            if step >= STEPS - 4:
-                ring_sent(step, 1)
-            ring_sent(step, 2)
-            last_sent(step)
-            gather_sent(step)
+            ring_sent(step, 1)
+        all_sent(STEPS - 1)
         router_sent()
 
 
@@ -478,7 +558,7 @@
     tree = scratch()
     names = tuple(tree)
     hbm, vmem = pl.BlockSpec(memory_space=pltpu.HBM), pl.BlockSpec(memory_space=pltpu.VMEM)
-    return pl.pallas_call(
+    fresh = pl.pallas_call(
         lambda *refs: kernel(names, *refs),
         out_shape=tuple(
             pltpu.VMEM(part.shape, F32) for part in (bucket_param, bucket_m, bucket_v, router_param, router_m, router_v)
@@ -504,6 +584,23 @@
         router_m,
         router_v,
     )
+    return pl.pallas_call(
+        store,
+        out_shape=tuple(jax.ShapeDtypeStruct(part.shape, F32) for part in fresh),
+        in_specs=[vmem] * 6,
+        out_specs=(hbm,) * 6,
+        scratch_shapes=[pltpu.SemaphoreType.DMA((6,))],
+        compiler_params=pltpu.CompilerParams(vmem_limit_bytes=1024 * 1024),
+        name="store",
+    )(*(pltpu.with_memory_space_constraint(part, pltpu.VMEM) for part in fresh))
+
+
+def store(*refs):
+    copies = [pltpu.make_async_copy(refs[n], refs[6 + n], refs[12].at[n]) for n in range(6)]
+    for copy in copies:
+        copy.start()
+    for copy in copies:
+        copy.wait()
 
 
 def solution(mesh):

time: 138 us -> 113 us (0.82)
  Pallas kernels: 131 us -> 112 us
  local copies, waits for them, and re-layouts: 5.75 us -> 0 us
    pallas_call x1, Pallas kernels: 131 us -> 109 us  [on_device(): pl.pallas_call(lambda *refs: kernel(names, *refs), out_shape=tuple((pltpu...]
    unnamed x6 -> x0, local copies, waits for them, and re-layouts: 5.75 us -> none
    pallas_call x0 -> x1, Pallas kernels: none -> 2.76 us  [on_device(): pl.pallas_call(store, out_shape=tuple((jax.ShapeDtypeStruct(part.shape, F...]
where the time goes in v3:
time: 113 us
  Pallas kernels  112 us (99%)
    pallas_call x1, Pallas kernels, on_device(): pl.pallas_call(lambda *refs: kernel(names, *refs), out_shape=tuple((pltpu...  109 us
    pallas_call x1, Pallas kernels, on_device(): pl.pallas_call(store, out_shape=tuple((jax.ShapeDtypeStruct(part.shape, F...  2.76 us

profile of v3, /device:TPU:0, one launch (start us, length us, event | category | flops | bytes accessed | tf_op | source)
XLA Modules:
  0.0 112.7 jit_solution(18079958637169603213)
XLA Ops:
  0.6 109.3 %reduce.1 = (f32[4,128,1024]{2,1,0:T(8,128)S(1)}, f32[4,128,1024]{2,1,0:T(8,128)S(1)}, f32[4,128,1024]{2,1,0:T(8,128)S(1)}, f32[2,1024]{1,0:T(2,128)S(1)}, f32[2,1024]{1,0:T(2,128)S(1)}, /*index=5*/f32[2,1024]{1,0:T(2,128)S(1)}) custom-call(s32[32]{0:T(128)} %refs_0_.1, bf16[8,1024]{1,0:T(8,128)(2,1)} %refs_1_.1, bf16[1024,4096]{1,0:T(8,128)(2,1)} %refs_2_.1, ...), custom_call_target="tpu_custom_call" | custom-call | flops 17200001024 | bytes 24000000 | tf_op jit(solution)/shard_map/reduce/pallas_call | solution.py:561
  110.0 2.8 %store.1 = (f32[4,128,1024]{2,1,0:T(8,128)}, f32[4,128,1024]{2,1,0:T(8,128)}, f32[4,128,1024]{2,1,0:T(8,128)}, f32[2,1024]{1,0:T(2,128)}, f32[2,1024]{1,0:T(2,128)}, /*index=5*/f32[2,1024]{1,0:T(2,128)}) custom-call(f32[4,128,1024]{2,1,0:T(8,128)S(1)} %get-tuple-element.12.refs_0_, f32[4,128,1024]{2,1,0:T(8,128)S(1)} %get-tuple-element.13.refs_1_, ...), custom_call_target="tpu_custom_call" | custom-call | tf_op jit(solution)/shard_map/store/pallas_call | solution.py:587

commit v4 on v3

--- a/solution.py
+++ b/solution.py
@@ -28,7 +28,9 @@
 W = 128
 OWN = 4
 SENT = 2
+RING = 4
 DIRECT = (STEPS - 1,)
+DIRECT_GATHER = (STEPS - 3, STEPS - 2, STEPS - 1)
 
 
 def adamw(grad, param, moment, second):
@@ -44,7 +46,8 @@
         "acts": pltpu.VMEM((16, 1024, BLOCK_ROWS), jnp.bfloat16),
         "grads0": pltpu.VMEM((2, 1024, HALF), jnp.bfloat16),
         "grads1": pltpu.VMEM((2, 1024, HALF), jnp.bfloat16),
-        "turned": pltpu.VMEM((BLOCK_ROWS, 1024), jnp.bfloat16),
+        "turned0": pltpu.VMEM((BLOCK_ROWS, 1024), jnp.bfloat16),
+        "turned1": pltpu.VMEM((BLOCK_ROWS, 1024), jnp.bfloat16),
         "out": pltpu.VMEM((BUCKETS, 2, 2, 4, 16, HALF), F32),
         "rt": pltpu.VMEM((2, 4, 2, 1, 2048), F32),
         "rx": pltpu.VMEM((4, 2, 1, 2048), F32),
@@ -52,22 +55,21 @@
         "rxy": pltpu.VMEM((4, 1, 2048), F32),
         "rxz": pltpu.VMEM((4, 1, 2048), F32),
         "ry": pltpu.VMEM((2, 1, 2048), F32),
-        "load_sem": pltpu.SemaphoreType.DMA((20,)),
+        "load_sem": pltpu.SemaphoreType.DMA((3,)),
         "state_sem": pltpu.SemaphoreType.DMA((3,)),
-        "x_send": pltpu.SemaphoreType.DMA((STEPS, 3)),
-        "x_recv": pltpu.SemaphoreType.DMA((STEPS, 3)),
-        "p1_send": pltpu.SemaphoreType.DMA((STEPS, 3, 6)),
-        "p1_recv": pltpu.SemaphoreType.DMA((STEPS, 3, 6)),
-        "p2_send": pltpu.SemaphoreType.DMA((STEPS, 3, 6)),
-        "p2_recv": pltpu.SemaphoreType.DMA((STEPS, 3, 6)),
-        "p3_send": pltpu.SemaphoreType.DMA((STEPS, 3, 3)),
-        "p3_recv": pltpu.SemaphoreType.DMA((STEPS, 3, 3)),
-        "ag_send": pltpu.SemaphoreType.DMA((STEPS, 5)),
-        "ag_recv": pltpu.SemaphoreType.DMA((STEPS, 5)),
-        "d_send": pltpu.SemaphoreType.DMA((STEPS, 7)),
-        "d_recv": pltpu.SemaphoreType.DMA((STEPS, 7)),
-        "r_send": pltpu.SemaphoreType.DMA((10,)),
-        "r_recv": pltpu.SemaphoreType.DMA((10,)),
+        "x_send": pltpu.SemaphoreType.DMA((SENT, 3)),
+        "x_recv": pltpu.SemaphoreType.DMA((SENT, 3)),
+        "p1_send": pltpu.SemaphoreType.DMA((RING, 3)),
+        "p1_recv": pltpu.SemaphoreType.DMA((RING, 3, 2)),
+        "p2_send": pltpu.SemaphoreType.DMA((RING, 3)),
+        "p2_recv": pltpu.SemaphoreType.DMA((RING, 3, 2)),
+        "p3_send": pltpu.SemaphoreType.DMA((RING, 3)),
+        "p3_recv": pltpu.SemaphoreType.DMA((RING, 3)),
+        "ag_send": pltpu.SemaphoreType.DMA((RING, 3)),
+        "ag_recv": pltpu.SemaphoreType.DMA((RING, 5)),
+        "d_recv": pltpu.SemaphoreType.DMA((3, 7)),
+        "r_send": pltpu.SemaphoreType.DMA((4,)),
+        "r_recv": pltpu.SemaphoreType.DMA((8,)),
     }
     for q in range(3):
         r = ROWS[q]
@@ -119,7 +121,7 @@
             pltpu.make_async_copy(
                 part.at[:, half * HALF : (half + 1) * HALF],
                 ref[f"grads{half}"].at[n],
-                ref["load_sem"].at[16 + half * 2 + n],
+                ref["load_sem"].at[1 + half],
             )
             for n, part in enumerate((keys_hbm, values_hbm))
         ]
@@ -128,7 +130,7 @@
     for i in range(16):
         loads.append(
             pltpu.make_async_copy(
-                acts_hbm.at[:, i * BLOCK_ROWS : (i + 1) * BLOCK_ROWS], ref["acts"].at[i], ref["load_sem"].at[i]
+                acts_hbm.at[:, i * BLOCK_ROWS : (i + 1) * BLOCK_ROWS], ref["acts"].at[i], ref["load_sem"].at[0]
             )
         )
     late_loads = grad_loads(1)
@@ -157,24 +159,41 @@
             send(
                 ref[f"sent{q}"].at[(step % SENT,) + spot],
                 ref[f"xr{q}"].at[(step % 4,) + spot],
-                ref["x_send"].at[step, q],
-                ref["x_recv"].at[step, q],
+                ref["x_send"].at[step % SENT, q],
+                ref["x_recv"].at[step % SENT, q],
                 sibling,
             )
 
+    def turn(step, j, into):
+        block = order[step // 2 * 8 + j] % 16
+        for h, side in enumerate((core, 1 - core)):
+            columns = ref["acts"][block, :, pl.ds(pl.multiple_of(side * 128, 128), 128)]
+            into[h * 128 : (h + 1) * 128] = columns.T
+
     def matmul(step, first, last):
         bucket, par = step // 2, step % 2
-
-        def body(j, carry):
+        turn(step, first, ref["turned0"])
+
+        def body(pair, carry):
+            j = first + pair * 2
+
+            @pl.when(pair > 0)
+            def _():
+                exchange(step, j - 1)
+
+            dots(step, j, 0, j + 1)
+            exchange(step, j)
+            dots(step, j + 1, 1, jnp.minimum(j + 2, 7))
+            return carry
+
+        def dots(step, j, now, later):
             slot_y, slot_x = j // 4, j % 4
             block = order[bucket * 8 + j]
-            for h, side in enumerate((core, 1 - core)):
-                columns = ref["acts"][block % 16, :, pl.ds(pl.multiple_of(side * 128, 128), 128)]
-                ref["turned"][h * 128 : (h + 1) * 128] = columns.T
+            turn(step, later, ref[f"turned{1 - now}"])
             for n in range(2):
                 lo = n * 256
                 piece = jnp.dot(
-                    ref["turned"][...],
+                    ref[f"turned{now}"][...],
                     ref[f"grads{par}"][block // 16, :, lo : lo + 256],
                     preferred_element_type=F32,
                 )
@@ -194,19 +213,13 @@
                                     at = ((slot_x, k, y), (y, slot_x, k), (k, y, slot_x))[q]
                                     ref[f"{dst}{q}"][(slot,) + at + (pl.ds(row, count),)] = value
 
-            @pl.when(j > first)
-            def _():
-                exchange(step, j - 1)
-
-            return carry
-
-        lax.fori_loop(first, last, body, 0)
+        lax.fori_loop(0, (last - first) // 2, body, 0)
         exchange(step, last - 1)
 
     def add_sibling(step):
         for q in range(3):
             own, xr = ref[f"own{q}"], ref[f"xr{q}"]
-            wait_recv(xr.at[step % 4], ref["x_recv"].at[step, q])
+            wait_recv(xr.at[step % 4], ref["x_recv"].at[step % SENT, q])
 
             def body(d, carry):
                 own[step % OWN, d] = own[step % OWN, d] + xr[step % 4, d]
@@ -220,6 +233,9 @@
         at = lambda d, h: (slot, d, pl.ds(2 * h, 2))
         into = (lambda m: (step % 4, m)) if phase == 1 else (lambda m: (step, pl.ds(2 * m, 2)))
         return src, at, recv, into
+
+    def group(step, phase, first, count):
+        return (step % 4, pl.ds(first, count)) if phase == 1 else (step, pl.ds(2 * first, 2 * count))
 
     def ring_send(step, q, phase, m, where, delta):
         src, at, recv, into = views(step, q, phase)
@@ -228,8 +244,8 @@
         send(
             src.at[at((place[dim] + d) % 4, h)],
             recv.at[into(m)],
-            ref[f"p{phase}_send"].at[step, q, m],
-            ref[f"p{phase}_recv"].at[step, q, m],
+            ref[f"p{phase}_send"].at[step % RING, q],
+            ref[f"p{phase}_recv"].at[step % RING, q, int(m > 1)],
             along(dim, delta),
         )
 
@@ -247,8 +263,8 @@
         for q in range(3):
             src, at, recv, into = views(step, q, phase)
             here = place[DIMS[q][phase - 1]]
+            wait_recv(recv.at[group(step, phase, 0, 2)], ref[f"p{phase}_recv"].at[step % RING, q, 0])
             for m, d, h in ((0, 1, 0), (1, 3, 1)):
-                wait_recv(recv.at[into(m)], ref[f"p{phase}_recv"].at[step, q, m])
                 spot = at((here + d) % 4, h)
                 src[spot] = src[spot] + recv[into(m)]
                 ring_send(step, q, phase, 4 + m, (d, h), d)
@@ -257,9 +273,8 @@
         for q in range(3):
             src, at, recv, into = views(step, q, phase)
             here = place[DIMS[q][phase - 1]]
+            wait_recv(recv.at[group(step, phase, 2, 4)], ref[f"p{phase}_recv"].at[step % RING, q, 1])
             for h, arrived in ((0, (3, 4)), (1, (2, 5))):
-                for m in arrived:
-                    wait_recv(recv.at[into(m)], ref[f"p{phase}_recv"].at[step, q, m])
                 spot = at(here, h)
                 total = src[spot] + recv[into(arrived[0])] + recv[into(arrived[1])]
                 if phase == 1:
@@ -269,9 +284,8 @@
 
     def ring_sent(step, phase):
         for q in range(3):
-            _, _, recv, into = views(step, q, phase)
-            for m in range(6):
-                wait_send(recv.at[into(m)], ref[f"p{phase}_send"].at[step, q, m])
+            recv = views(step, q, phase)[2]
+            wait_send(recv.at[group(step, phase, 0, 6)], ref[f"p{phase}_send"].at[step % RING, q])
 
     def second_start(step):
         for m, delta in enumerate((2, 1, 3)):
@@ -280,29 +294,23 @@
                 send(
                     ref[f"q{q}"].at[step, (place[dim] + delta) % 4],
                     ref[f"rb{q}"].at[step, pl.ds(4 * m, 4)],
-                    ref["p2_send"].at[step, q, m],
-                    ref["p2_recv"].at[step, q, m],
+                    ref["p2_send"].at[step % RING, q],
+                    ref["p2_recv"].at[step % RING, q, 0],
                     along(dim, delta),
                 )
 
     def second_end(step):
         for q in range(3):
             rb, here = ref[f"rb{q}"], place[DIMS[q][1]]
-            for m in range(3):
-                wait_recv(rb.at[step, pl.ds(4 * m, 4)], ref["p2_recv"].at[step, q, m])
+            wait_recv(rb.at[step], ref["p2_recv"].at[step % RING, q, 0])
             total = ref[f"q{q}"][step, here]
             for m in range(3):
                 total = total + rb[step, pl.ds(4 * m, 4)]
             ref[f"q{q}"][step, here] = total
 
-    def second_sent(step):
-        for q in range(3):
-            for m in range(3):
-                wait_send(ref[f"rb{q}"].at[step, pl.ds(4 * m, 4)], ref["p2_send"].at[step, q, m])
-
     def exchange_sent(step):
         for q in range(3):
-            wait_send(ref[f"xr{q}"].at[step % 4], ref["x_send"].at[step, q])
+            wait_send(ref[f"xr{q}"].at[step % 4], ref["x_send"].at[step % SENT, q])
 
     def last_start(step):
         for q in range(3):
@@ -312,8 +320,8 @@
                 send(
                     ref[f"q{q}"].at[step, place[second], (place[third] + delta) % 4],
                     ref[f"rc{q}"].at[step, m],
-                    ref["p3_send"].at[step, q, m],
-                    ref["p3_recv"].at[step, q, m],
+                    ref["p3_send"].at[step % RING, q],
+                    ref["p3_recv"].at[step % RING, q],
                     along(third, delta),
                 )
 
@@ -322,23 +330,21 @@
         for q in range(3):
             second, third = DIMS[q][1:]
             rc = ref[f"rc{q}"]
-            for m in range(3):
-                wait_recv(rc.at[step, m], ref["p3_recv"].at[step, q, m])
+            wait_recv(rc.at[step], ref["p3_recv"].at[step % RING, q])
             total = ref[f"q{q}"][step, place[second], place[third]] + rc[step, 0] + rc[step, 1] + rc[step, 2]
             for chunk, top, count, row in PARTS[q]:
                 ref["out"][b, par, yl, z, pl.ds(top, count), pl.ds(chunk * W, W)] = total[row : row + count]
 
     def last_sent(step):
         for q in range(3):
-            for m in range(3):
-                wait_send(ref[f"rc{q}"].at[step, m], ref["p3_send"].at[step, q, m])
+            wait_send(ref[f"rc{q}"].at[step], ref["p3_send"].at[step % RING, q])
 
     def gather_send(step, n, spot, to):
         out = ref["out"].at[(step // 2, step % 2) + spot]
-        send(out, out, ref["ag_send"].at[step, n], ref["ag_recv"].at[step, n], to)
-
-    def gather_wait(step, n, spot, which="ag_recv"):
-        wait_recv(ref["out"].at[(step // 2, step % 2) + spot], ref[which].at[step, n])
+        send(out, out, ref["ag_send"].at[step % RING, (n + 1) // 2], ref["ag_recv"].at[step % RING, n], to)
+
+    def gather_wait(step, n, spot):
+        wait_recv(ref["out"].at[(step // 2, step % 2) + spot], ref["ag_recv"].at[step % RING, n])
 
     both = pl.ds(0, 2)
 
@@ -359,17 +365,18 @@
     def gather_direct(step):
         b, par = step // 2, step % 2
         own = ref["out"].at[b, par, yl, z]
-        for n in (5, 1, 6, 2, 4, 0, 3):
+        for count, n in enumerate((5, 1, 6, 2, 4, 0, 3)):
             dy, dz = divmod(n + 1, 4)
             to = device(y=yh * 2 + (yl + dy) % 2, z=(z + dz) % 4)
-            send(own, own, ref["d_send"].at[step, n], ref["d_recv"].at[step, n], to)
+            sent = (0, 1, 1, 1, 1, 2, 2)[count]
+            send(own, own, ref["ag_send"].at[step % RING, sent], ref["d_recv"].at[STEPS - 1 - step, n], to)
 
     def gather_end(step):
-        if step in DIRECT:
+        if step in DIRECT_GATHER:
             for n in range(7):
                 dy, dz = divmod(n + 1, 4)
                 there = ref["out"].at[step // 2, step % 2, (yl + dy) % 2, (z - dz) % 4]
-                wait_recv(there, ref["d_recv"].at[step, n])
+                wait_recv(there, ref["d_recv"].at[STEPS - 1 - step, n])
         else:
             gather_wait(step, 3, (0, (z + 2) % 4))
             gather_wait(step, 4, (1, (z + 2) % 4))
@@ -387,12 +394,9 @@
         lax.fori_loop(0, 8, body, 0)
 
     def gather_sent(step):
-        if step in DIRECT:
-            for n in range(7):
-                wait_send(ref["out"].at[step // 2, step % 2, yl, z], ref["d_send"].at[step, n])
-            return
-        for n, spot in enumerate(((yl, z), (both, z), (both, z), (0, z), (1, z))):
-            gather_wait(step, n, spot, "ag_send")
+        out = ref["out"].at[step // 2, step % 2]
+        for n, part in enumerate((out.at[0, 0], out.at[0], out.at[both, 0])):
+            wait_send(part, ref["ag_send"].at[step % RING, n])
 
     def state_start():
         for load in state_loads:
@@ -403,10 +407,10 @@
             load.wait()
 
     def router_send(n, src, dst, to):
-        send(src, dst, ref["r_send"].at[n], ref["r_recv"].at[n], to)
+        send(src, dst, ref["r_send"].at[(n + 2) // 3], ref["r_recv"].at[max(n - 2, min(n, 1))], to)
 
     def router_wait(n, dst):
-        wait_recv(dst, ref["r_recv"].at[n])
+        wait_recv(dst, ref["r_recv"].at[max(n - 2, min(n, 1))])
 
     def router_0():
         router_send(0, ref["rt"].at[1 - core], ref["rx"], sibling)
@@ -418,8 +422,7 @@
             router_send(1 + m, ref["rt"].at[core, (x + delta) % 4], ref["rxx"].at[m], along("x", delta))
 
     def router_2():
-        for m in range(3):
-            router_wait(1 + m, ref["rxx"].at[m])
+        router_wait(1, ref["rxx"])
         ref["ry"][...] = ref["rt"][core, x] + ref["rxx"][0] + ref["rxx"][1] + ref["rxx"][2]
         here = place["y"]
         ref["rxy"][here] = ref["ry"][yh]
@@ -448,10 +451,9 @@
 
     def router_sent():
         wait_send(ref["rx"], ref["r_send"].at[0])
-        for m in range(3):
-            wait_send(ref["rxx"].at[m], ref["r_send"].at[1 + m])
-            wait_send(ref["rxy"].at[m], ref["r_send"].at[4 + m])
-            wait_send(ref["rxz"].at[m], ref["r_send"].at[7 + m])
+        wait_send(ref["rxx"], ref["r_send"].at[1])
+        wait_send(ref["rxy"].at[pl.ds(0, 3)], ref["r_send"].at[2])
+        wait_send(ref["rxz"].at[pl.ds(0, 3)], ref["r_send"].at[3])
 
     router_stages = {0: router_0, 1: router_1, 2: router_2, 3: router_3, 4: router_4}
 
@@ -463,25 +465,15 @@
         return 0 <= step < STEPS
 
     with jax.named_scope("loads"):
-        for load in loads:
-            load.wait()
+        wait_recv(ref["grads0"], ref["load_sem"].at[1])
+        wait_recv(ref["acts"], ref["load_sem"].at[0])
     with jax.named_scope("barrier"):
         pl.semaphore_wait(barrier, len(peers))
     run(matmul, 0, 0, 8)
-    run(router_term)
-    run(router_0)
     run(add_sibling, 0)
     run(ring_start, 0, 1)
-    for load in late_loads:
-        load.wait()
-    state_start()
 
     def all_sent(step):
-        if step in DIRECT:
-            second_sent(step)
-        else:
-            ring_sent(step, 2)
-        last_sent(step)
         gather_sent(step)
 
     for i in range(STEPS + 5):
@@ -489,6 +481,11 @@
             run(ring_relay, i - 2, 2)
         if live(i):
             run(ring_next, i, 1)
+        if i == 0:
+            run(router_term)
+            run(router_0)
+            wait_recv(ref["grads1"], ref["load_sem"].at[2])
+            state_start()
         if live(i + 1):
             if live(i - 1):
                 run(exchange_sent, i - 1)
@@ -517,13 +514,15 @@
             run(ring_start, i + 1, 1)
         if live(i - 3):
             run(last_end, i - 3)
-            if i - 3 in DIRECT:
+            run(ring_sent, i - 3, 2)
+            run(last_sent, i - 3)
+            if i - 3 in DIRECT_GATHER:
                 run(gather_direct, i - 3)
             else:
                 run(gather_partner, i - 3)
-        if live(i - 4) and i - 4 not in DIRECT:
+        if live(i - 4) and i - 4 not in DIRECT_GATHER:
             run(gather_start, i - 4)
-        if live(i - 5) and i - 5 not in DIRECT:
+        if live(i - 5) and i - 5 not in DIRECT_GATHER:
             run(gather_relay, i - 5)
         if i + 1 in router_stages:
             run(router_stages[i + 1])

time: 113 us -> 105 us (0.929)
  Pallas kernels: 112 us -> 104 us
    pallas_call x1, Pallas kernels: 109 us -> 101 us  [on_device(): pl.pallas_call(lambda *refs: kernel(names, *refs), out_shape=tuple((pltpu...]
where the time goes in v4:
time: 105 us
  Pallas kernels  104 us (99%)
    pallas_call x1, Pallas kernels, on_device(): pl.pallas_call(lambda *refs: kernel(names, *refs), out_shape=tuple((pltpu...  101 us
    pallas_call x1, Pallas kernels, on_device(): pl.pallas_call(store, out_shape=tuple((jax.ShapeDtypeStruct(part.shape, F...  2.76 us

profile of v4, /device:TPU:0, one launch (start us, length us, event | category | flops | bytes accessed | tf_op | source)
XLA Modules:
  0.0 104.8 jit_solution(12063258745474262590)
XLA Ops:
  0.6 101.3 %reduce.1 = (f32[4,128,1024]{2,1,0:T(8,128)S(1)}, f32[4,128,1024]{2,1,0:T(8,128)S(1)}, f32[4,128,1024]{2,1,0:T(8,128)S(1)}, f32[2,1024]{1,0:T(2,128)S(1)}, f32[2,1024]{1,0:T(2,128)S(1)}, /*index=5*/f32[2,1024]{1,0:T(2,128)S(1)}) custom-call(s32[32]{0:T(128)} %refs_0_.1, bf16[8,1024]{1,0:T(8,128)(2,1)} %refs_1_.1, bf16[1024,4096]{1,0:T(8,128)(2,1)} %refs_2_.1, ...), custom_call_target="tpu_custom_call" | custom-call | flops 17200001024 | bytes 24000000 | tf_op jit(solution)/shard_map/reduce/pallas_call | solution.py:560
  101.9 2.8 %store.1 = (f32[4,128,1024]{2,1,0:T(8,128)}, f32[4,128,1024]{2,1,0:T(8,128)}, f32[4,128,1024]{2,1,0:T(8,128)}, f32[2,1024]{1,0:T(2,128)}, f32[2,1024]{1,0:T(2,128)}, /*index=5*/f32[2,1024]{1,0:T(2,128)}) custom-call(f32[4,128,1024]{2,1,0:T(8,128)S(1)} %get-tuple-element.12.refs_0_, f32[4,128,1024]{2,1,0:T(8,128)S(1)} %get-tuple-element.13.refs_1_, ...), custom_call_target="tpu_custom_call" | custom-call | tf_op jit(solution)/shard_map/store/pallas_call | solution.py:586

commit v5 on v4

--- a/solution.py
+++ b/solution.py
@@ -9,6 +9,7 @@
 BLOCK_ROWS = 256
 STEPS = 8
 HALF = 512
+DEEP = 512
 
 beta_first = 0.9
 beta_second = 0.95
@@ -30,7 +31,7 @@
 SENT = 2
 RING = 4
 DIRECT = (STEPS - 1,)
-DIRECT_GATHER = (STEPS - 3, STEPS - 2, STEPS - 1)
+DIRECT_GATHER = (STEPS - 2, STEPS - 1)
 
 
 def adamw(grad, param, moment, second):
@@ -43,9 +44,12 @@
 
 def scratch():
     tree = {
-        "acts": pltpu.VMEM((16, 1024, BLOCK_ROWS), jnp.bfloat16),
-        "grads0": pltpu.VMEM((2, 1024, HALF), jnp.bfloat16),
-        "grads1": pltpu.VMEM((2, 1024, HALF), jnp.bfloat16),
+        "acts0": pltpu.VMEM((16, DEEP, BLOCK_ROWS), jnp.bfloat16),
+        "acts1": pltpu.VMEM((16, DEEP, BLOCK_ROWS), jnp.bfloat16),
+        "grads00": pltpu.VMEM((2, DEEP, HALF), jnp.bfloat16),
+        "grads01": pltpu.VMEM((2, DEEP, HALF), jnp.bfloat16),
+        "grads10": pltpu.VMEM((2, DEEP, HALF), jnp.bfloat16),
+        "grads11": pltpu.VMEM((2, DEEP, HALF), jnp.bfloat16),
         "turned0": pltpu.VMEM((BLOCK_ROWS, 1024), jnp.bfloat16),
         "turned1": pltpu.VMEM((BLOCK_ROWS, 1024), jnp.bfloat16),
         "out": pltpu.VMEM((BUCKETS, 2, 2, 4, 16, HALF), F32),
@@ -55,7 +59,7 @@
         "rxy": pltpu.VMEM((4, 1, 2048), F32),
         "rxz": pltpu.VMEM((4, 1, 2048), F32),
         "ry": pltpu.VMEM((2, 1, 2048), F32),
-        "load_sem": pltpu.SemaphoreType.DMA((3,)),
+        "load_sem": pltpu.SemaphoreType.DMA((6,)),
         "state_sem": pltpu.SemaphoreType.DMA((3,)),
         "x_send": pltpu.SemaphoreType.DMA((SENT, 3)),
         "x_recv": pltpu.SemaphoreType.DMA((SENT, 3)),
@@ -116,26 +120,24 @@
 
     wait_send = wait_recv
 
-    def grad_loads(half):
-        return [
+    def grad_load(half, k):
+        for n, part in enumerate((keys_hbm, values_hbm)):
             pltpu.make_async_copy(
-                part.at[:, half * HALF : (half + 1) * HALF],
-                ref[f"grads{half}"].at[n],
-                ref["load_sem"].at[1 + half],
-            )
-            for n, part in enumerate((keys_hbm, values_hbm))
-        ]
-
-    loads = grad_loads(0)
-    for i in range(16):
-        loads.append(
+                part.at[pl.ds(k * DEEP, DEEP), pl.ds(half * HALF, HALF)],
+                ref[f"grads{half}{k}"].at[n],
+                ref["load_sem"].at[2 + half * 2 + k],
+            ).start()
+
+    for k in range(2):
+        grad_load(0, k)
+        for i in range(16):
             pltpu.make_async_copy(
-                acts_hbm.at[:, i * BLOCK_ROWS : (i + 1) * BLOCK_ROWS], ref["acts"].at[i], ref["load_sem"].at[0]
-            )
-        )
-    late_loads = grad_loads(1)
-    for load in loads + late_loads:
-        load.start()
+                acts_hbm.at[pl.ds(k * DEEP, DEEP), pl.ds(i * BLOCK_ROWS, BLOCK_ROWS)],
+                ref[f"acts{k}"].at[i],
+                ref["load_sem"].at[k],
+            ).start()
+    for k in range(2):
+        grad_load(1, k)
     state_loads = [pltpu.make_async_copy(state_hbm[n], state[n], ref["state_sem"].at[n]) for n in range(3)]
 
     barrier = pltpu.get_barrier_semaphore()
@@ -145,7 +147,8 @@
 
     def router_term():
         for i in range(16):
-            term = jnp.dot(logits[...], ref["acts"][i], preferred_element_type=F32)
+            block = jnp.concatenate([ref["acts0"][i], ref["acts1"][i]], axis=0)
+            term = jnp.dot(logits[...], block, preferred_element_type=F32)
             for e in range(8):
                 ref["rt"][i // 8, e % 4, e // 4, :, pl.ds((i % 8) * 256, 256)] = term[e : e + 1, :]
 
@@ -164,37 +167,42 @@
                 sibling,
             )
 
-    def turn(step, j, into):
+    def turn(step, j, into, halves):
         block = order[step // 2 * 8 + j] % 16
         for h, side in enumerate((core, 1 - core)):
-            columns = ref["acts"][block, :, pl.ds(pl.multiple_of(side * 128, 128), 128)]
-            into[h * 128 : (h + 1) * 128] = columns.T
-
-    def matmul(step, first, last):
+            for k in halves:
+                columns = ref[f"acts{k}"][block, :, pl.ds(pl.multiple_of(side * 128, 128), 128)]
+                into[h * 128 : (h + 1) * 128, k * DEEP : (k + 1) * DEEP] = columns.T
+
+    def matmul(step, first, last, halves=(0, 1)):
         bucket, par = step // 2, step % 2
-        turn(step, first, ref["turned0"])
+        turn(step, first, ref["turned0"], halves)
 
         def body(pair, carry):
             j = first + pair * 2
-
-            @pl.when(pair > 0)
-            def _():
-                exchange(step, j - 1)
+            if 1 in halves:
+
+                @pl.when(pair > 0)
+                def _():
+                    exchange(step, j - 1)
 
             dots(step, j, 0, j + 1)
-            exchange(step, j)
+            if 1 in halves:
+                exchange(step, j)
             dots(step, j + 1, 1, jnp.minimum(j + 2, 7))
             return carry
 
         def dots(step, j, now, later):
             slot_y, slot_x = j // 4, j % 4
             block = order[bucket * 8 + j]
-            turn(step, later, ref[f"turned{1 - now}"])
+            turn(step, later, ref[f"turned{1 - now}"], halves)
             for n in range(2):
                 lo = n * 256
                 piece = jnp.dot(
-                    ref[f"turned{now}"][...],
-                    ref[f"grads{par}"][block // 16, :, lo : lo + 256],
+                    ref[f"turned{now}"][:, halves[0] * DEEP : (halves[-1] + 1) * DEEP],
+                    jnp.concatenate(
+                        [ref[f"grads{par}{k}"][block // 16, :, lo : lo + 256] for k in halves], axis=0
+                    ),
                     preferred_element_type=F32,
                 )
                 for h in range(2):
@@ -211,10 +219,14 @@
                                     start = h * 128 + l * 64 + k * 16 + top
                                     value = piece[start : start + count, left : left + W]
                                     at = ((slot_x, k, y), (y, slot_x, k), (k, y, slot_x))[q]
-                                    ref[f"{dst}{q}"][(slot,) + at + (pl.ds(row, count),)] = value
+                                    spot = (slot,) + at + (pl.ds(row, count),)
+                                    if halves == (1,):
+                                        value = ref[f"{dst}{q}"][spot] + value
+                                    ref[f"{dst}{q}"][spot] = value
 
         lax.fori_loop(0, (last - first) // 2, body, 0)
-        exchange(step, last - 1)
+        if 1 in halves:
+            exchange(step, last - 1)
 
     def add_sibling(step):
         for q in range(3):
@@ -458,33 +470,62 @@
     router_stages = {0: router_0, 1: router_1, 2: router_2, 3: router_3, 4: router_4}
 
     def run(stage, *args):
-        with jax.named_scope(f"{stage.__name__}#s={'_'.join(map(str, args))}"):
+        with jax.named_scope(f"{stage.__name__}#s={'_'.join(map(str, args)).replace(' ', '')}"):
             stage(*args)
 
     def live(step):
         return 0 <= step < STEPS
 
-    with jax.named_scope("loads"):
-        wait_recv(ref["grads0"], ref["load_sem"].at[1])
-        wait_recv(ref["acts"], ref["load_sem"].at[0])
+    def loaded(k):
+        wait_recv(ref[f"grads0{k}"], ref["load_sem"].at[2 + k])
+        wait_recv(ref[f"acts{k}"], ref["load_sem"].at[k])
+
+    run(loaded, 0)
+    run(matmul, 0, 0, 8, (0,))
+    run(loaded, 1)
     with jax.named_scope("barrier"):
         pl.semaphore_wait(barrier, len(peers))
-    run(matmul, 0, 0, 8)
+    run(matmul, 0, 0, 8, (1,))
     run(add_sibling, 0)
     run(ring_start, 0, 1)
 
-    def all_sent(step):
-        gather_sent(step)
-
-    for i in range(STEPS + 5):
-        if live(i - 2) and i - 2 not in DIRECT:
+    def second(step):
+        run(ring_end, step, 1)
+        if step in DIRECT:
+            run(second_start, step)
+        else:
+            run(ring_start, step, 2)
+            run(ring_next, step, 2)
+
+    def third(step):
+        if step in DIRECT:
+            run(second_end, step)
+        else:
+            run(ring_end, step, 2)
+        run(last_start, step)
+
+    def spread(step):
+        run(last_end, step)
+        ring_sent(step, 2)
+        last_sent(step)
+        if step in DIRECT_GATHER:
+            run(gather_direct, step)
+        else:
+            run(gather_partner, step)
+
+    def finish(step):
+        run(gather_end, step)
+        run(gather_sent, step)
+
+    for i in range(STEPS):
+        if live(i - 2):
             run(ring_relay, i - 2, 2)
-        if live(i):
-            run(ring_next, i, 1)
+        run(ring_next, i, 1)
         if i == 0:
             run(router_term)
             run(router_0)
-            wait_recv(ref["grads1"], ref["load_sem"].at[2])
+            for k in range(2):
+                wait_recv(ref[f"grads1{k}"], ref["load_sem"].at[4 + k])
             state_start()
         if live(i + 1):
             if live(i - 1):
@@ -493,51 +534,49 @@
                 run(ring_sent, i - 3, 1)
             run(matmul, i + 1, 0, 4)
         if live(i - 1):
-            run(ring_end, i - 1, 1)
-            if i - 1 in DIRECT:
-                run(second_start, i - 1)
-            else:
-                run(ring_start, i - 1, 2)
-                run(ring_next, i - 1, 2)
+            second(i - 1)
+        if live(i - 3):
+            spread(i - 3)
+        if live(i - 4):
+            run(gather_start, i - 4)
         if live(i + 1):
             run(matmul, i + 1, 4, 8)
-        if live(i):
-            run(ring_relay, i, 1)
+        run(ring_relay, i, 1)
         if live(i - 2):
-            if i - 2 in DIRECT:
-                run(second_end, i - 2)
-            else:
-                run(ring_end, i - 2, 2)
-            run(last_start, i - 2)
+            third(i - 2)
         if live(i + 1):
             run(add_sibling, i + 1)
             run(ring_start, i + 1, 1)
-        if live(i - 3):
-            run(last_end, i - 3)
-            run(ring_sent, i - 3, 2)
-            run(last_sent, i - 3)
-            if i - 3 in DIRECT_GATHER:
-                run(gather_direct, i - 3)
-            else:
-                run(gather_partner, i - 3)
-        if live(i - 4) and i - 4 not in DIRECT_GATHER:
-            run(gather_start, i - 4)
-        if live(i - 5) and i - 5 not in DIRECT_GATHER:
-            run(gather_relay, i - 5)
+        if live(i - 4) and i < STEPS - 1:
+            run(gather_relay, i - 4)
         if i + 1 in router_stages:
             run(router_stages[i + 1])
-        if i == 5:
-            run(state_end)
-        if live(i - 6):
-            run(gather_end, i - 6)
-            run(all_sent, i - 6)
-    run(gather_end, STEPS - 1)
+        if live(i - 5) and i < STEPS - 1:
+            if i == 5:
+                run(state_end)
+            finish(i - 5)
+    last = STEPS - 1
+    run(ring_relay, last - 1, 2)
+    run(gather_relay, last - 4)
+    run(gather_start, last - 3)
+    second(last)
+    third(last - 1)
+    spread(last - 2)
+    run(gather_relay, last - 3)
+    finish(last - 5)
+    third(last)
+    run(gather_start, last - 2)
+    spread(last - 1)
+    finish(last - 4)
+    spread(last)
+    run(gather_relay, last - 2)
+    for step in range(last - 3, last + 1):
+        finish(step)
     with jax.named_scope("ending"):
         for step in range(STEPS - 4, STEPS):
             if step >= STEPS - 2:
                 exchange_sent(step)
             ring_sent(step, 1)
-        all_sent(STEPS - 1)
         router_sent()
 
 
@@ -588,14 +627,19 @@
         out_shape=tuple(jax.ShapeDtypeStruct(part.shape, F32) for part in fresh),
         in_specs=[vmem] * 6,
         out_specs=(hbm,) * 6,
-        scratch_shapes=[pltpu.SemaphoreType.DMA((6,))],
+        scratch_shapes=[pltpu.SemaphoreType.DMA((15,))],
         compiler_params=pltpu.CompilerParams(vmem_limit_bytes=1024 * 1024),
         name="store",
     )(*(pltpu.with_memory_space_constraint(part, pltpu.VMEM) for part in fresh))
 
 
 def store(*refs):
-    copies = [pltpu.make_async_copy(refs[n], refs[6 + n], refs[12].at[n]) for n in range(6)]
+    copies = []
+    for n in range(3):
+        copies.append((refs[3 + n], refs[9 + n]))
+        for b in range(BUCKETS):
+            copies.append((refs[n].at[b], refs[6 + n].at[b]))
+    copies = [pltpu.make_async_copy(src, dst, refs[12].at[n]) for n, (src, dst) in enumerate(copies)]
     for copy in copies:
         copy.start()
     for copy in copies:

time: 105 us -> 103 us (0.981)
  Pallas kernels: 104 us -> 102 us
    pallas_call x1, Pallas kernels: 101 us -> 99.3 us  [on_device(): pl.pallas_call(lambda *refs: kernel(names, *refs), out_shape=tuple((pltpu...]
where the time goes in v5:
time: 103 us
  Pallas kernels  102 us (99%)
    pallas_call x1, Pallas kernels, on_device(): pl.pallas_call(lambda *refs: kernel(names, *refs), out_shape=tuple((pltpu...  99.3 us
    pallas_call x1, Pallas kernels, on_device(): pl.pallas_call(store, out_shape=tuple((jax.ShapeDtypeStruct(part.shape, F...  2.79 us

profile of v5, /device:TPU:0, one launch (start us, length us, event | category | flops | bytes accessed | tf_op | source)
XLA Modules:
  0.0 102.9 jit_solution(3182382805427292467)
XLA Ops:
  0.6 99.3 %reduce.1 = (f32[4,128,1024]{2,1,0:T(8,128)S(1)}, f32[4,128,1024]{2,1,0:T(8,128)S(1)}, f32[4,128,1024]{2,1,0:T(8,128)S(1)}, f32[2,1024]{1,0:T(2,128)S(1)}, f32[2,1024]{1,0:T(2,128)S(1)}, /*index=5*/f32[2,1024]{1,0:T(2,128)S(1)}) custom-call(s32[32]{0:T(128)} %refs_0_.1, bf16[8,1024]{1,0:T(8,128)(2,1)} %refs_1_.1, bf16[1024,4096]{1,0:T(8,128)(2,1)} %refs_2_.1, ...), custom_call_target="tpu_custom_call" | custom-call | flops 17200001024 | bytes 24000000 | tf_op jit(solution)/shard_map/reduce/pallas_call | solution.py:599
  100.0 2.8 %store.1 = (f32[4,128,1024]{2,1,0:T(8,128)}, f32[4,128,1024]{2,1,0:T(8,128)}, f32[4,128,1024]{2,1,0:T(8,128)}, f32[2,1024]{1,0:T(2,128)}, f32[2,1024]{1,0:T(2,128)}, /*index=5*/f32[2,1024]{1,0:T(2,128)}) custom-call(f32[4,128,1024]{2,1,0:T(8,128)S(1)} %get-tuple-element.12.refs_0_, f32[4,128,1024]{2,1,0:T(8,128)S(1)} %get-tuple-element.13.refs_1_, ...), custom_call_target="tpu_custom_call" | custom-call | tf_op jit(solution)/shard_map/store/pallas_call | solution.py:625

commit v6 on v5

--- a/solution.py
+++ b/solution.py
@@ -61,6 +61,10 @@
         "ry": pltpu.VMEM((2, 1, 2048), F32),
         "load_sem": pltpu.SemaphoreType.DMA((6,)),
         "state_sem": pltpu.SemaphoreType.DMA((3,)),
+        "order": pltpu.SMEM((32,), jnp.int32),
+        "logits": pltpu.VMEM((8, 1024), jnp.bfloat16),
+        "router": pltpu.VMEM((3, 2, 1024), F32),
+        "small_sem": pltpu.SemaphoreType.DMA((5,)),
         "x_send": pltpu.SemaphoreType.DMA((SENT, 3)),
         "x_recv": pltpu.SemaphoreType.DMA((SENT, 3)),
         "p1_send": pltpu.SemaphoreType.DMA((RING, 3)),
@@ -71,7 +75,7 @@
         "p3_recv": pltpu.SemaphoreType.DMA((RING, 3)),
         "ag_send": pltpu.SemaphoreType.DMA((RING, 3)),
         "ag_recv": pltpu.SemaphoreType.DMA((RING, 5)),
-        "d_recv": pltpu.SemaphoreType.DMA((3, 7)),
+        "d_recv": pltpu.SemaphoreType.DMA((2, 7)),
         "r_send": pltpu.SemaphoreType.DMA((4,)),
         "r_recv": pltpu.SemaphoreType.DMA((8,)),
     }
@@ -87,8 +91,8 @@
     return tree
 
 
-def kernel(names, order, logits, acts_hbm, keys_hbm, values_hbm, *refs):
-    state_hbm, router_state = refs[0:3], refs[3:6]
+def kernel(names, order_hbm, logits_hbm, acts_hbm, keys_hbm, values_hbm, *refs):
+    state_hbm, router_hbm = refs[0:3], refs[3:6]
     state, router_new = refs[6:9], refs[9:12]
     refs = refs[12:]
     ref = dict(zip(names, refs))
@@ -128,6 +132,12 @@
                 ref["load_sem"].at[2 + half * 2 + k],
             ).start()
 
+    order, logits = ref["order"], ref["logits"]
+    router_state = [ref["router"].at[n] for n in range(3)]
+    small = [(order_hbm, order), (logits_hbm, logits)] + list(zip(router_hbm, router_state))
+    small = [pltpu.make_async_copy(src, dst, ref["small_sem"].at[n]) for n, (src, dst) in enumerate(small)]
+    for copy in small:
+        copy.start()
     for k in range(2):
         grad_load(0, k)
         for i in range(16):
@@ -481,6 +491,7 @@
         wait_recv(ref[f"acts{k}"], ref["load_sem"].at[k])
 
     run(loaded, 0)
+    small[0].wait()
     run(matmul, 0, 0, 8, (0,))
     run(loaded, 1)
     with jax.named_scope("barrier"):
@@ -522,6 +533,8 @@
             run(ring_relay, i - 2, 2)
         run(ring_next, i, 1)
         if i == 0:
+            for copy in small[1:]:
+                copy.wait()
             run(router_term)
             run(router_0)
             for k in range(2):
@@ -570,7 +583,7 @@
     finish(last - 4)
     spread(last)
     run(gather_relay, last - 2)
-    for step in range(last - 3, last + 1):
+    for step in (last - 3, last - 1, last, last - 2):
         finish(step)
     with jax.named_scope("ending"):
         for step in range(STEPS - 4, STEPS):
@@ -601,7 +614,7 @@
         out_shape=tuple(
             pltpu.VMEM(part.shape, F32) for part in (bucket_param, bucket_m, bucket_v, router_param, router_m, router_v)
         ),
-        in_specs=[pl.BlockSpec(memory_space=pltpu.SMEM), vmem] + [hbm] * 6 + [vmem] * 3,
+        in_specs=[hbm] * 11,
         out_specs=(vmem,) * 6,
         scratch_shapes=list(tree.values()),
         compiler_params=pltpu.CompilerParams(

time: 103 us -> 102 us (level)
    pallas_call x1, Pallas kernels: 99.3 us -> 97.7 us  [on_device(): pl.pallas_call(lambda *refs: kernel(names, *refs), out_shape=tuple((pltpu...]
where the time goes in v6:
time: 102 us; the launch traced here: 101 us
  Pallas kernels  101 us (99%)
    pallas_call x1, Pallas kernels, on_device(): pl.pallas_call(lambda *refs: kernel(names, *refs), out_shape=tuple((pltpu...  97.7 us
    pallas_call x1, Pallas kernels, on_device(): pl.pallas_call(store, out_shape=tuple((jax.ShapeDtypeStruct(part.shape, F...  2.79 us

profile of v6, /device:TPU:0, one launch (start us, length us, event | category | flops | bytes accessed | tf_op | source)
XLA Modules:
  0.0 101.3 jit_solution(14447676318270486889)
XLA Ops:
  0.6 97.7 %reduce.1 = (f32[4,128,1024]{2,1,0:T(8,128)S(1)}, f32[4,128,1024]{2,1,0:T(8,128)S(1)}, f32[4,128,1024]{2,1,0:T(8,128)S(1)}, f32[2,1024]{1,0:T(2,128)S(1)}, f32[2,1024]{1,0:T(2,128)S(1)}, /*index=5*/f32[2,1024]{1,0:T(2,128)S(1)}) custom-call(s32[32]{0:T(128)} %refs_0_.1, bf16[8,1024]{1,0:T(8,128)(2,1)} %refs_1_.1, bf16[1024,4096]{1,0:T(8,128)(2,1)} %refs_2_.1, ...), custom_call_target="tpu_custom_call" | custom-call | flops 17200001024 | bytes 24000000 | tf_op jit(solution)/shard_map/reduce/pallas_call | solution.py:612
  98.4 2.8 %store.1 = (f32[4,128,1024]{2,1,0:T(8,128)}, f32[4,128,1024]{2,1,0:T(8,128)}, f32[4,128,1024]{2,1,0:T(8,128)}, f32[2,1024]{1,0:T(2,128)}, f32[2,1024]{1,0:T(2,128)}, /*index=5*/f32[2,1024]{1,0:T(2,128)}) custom-call(f32[4,128,1024]{2,1,0:T(8,128)S(1)} %get-tuple-element.12.refs_0_, f32[4,128,1024]{2,1,0:T(8,128)S(1)} %get-tuple-element.13.refs_1_, ...), custom_call_target="tpu_custom_call" | custom-call | tf_op jit(solution)/shard_map/store/pallas_call | solution.py:638
